TPU v7x, 8 devices: a whole 2x2x1 slice. The times are simulated.
8 devices in a mesh: rep: 2 (over y, z), dp: 4 (over x, core).
Axes of the slice: x: 2, y: 2, z: 1, core: 2. Of those that a mesh axis runs over, the one named last changes fastest.
Arguments:
- x: bfloat16 [8, 2048, 768], P(('rep', 'dp')), parts along dimension 0
- dy: bfloat16 [8, 2048, 768], P(('rep', 'dp')), parts along dimension 0
- w_gate: bfloat16 [2, 768, 3072], replicated
- w_up: bfloat16 [2, 768, 3072], replicated
- w_down: bfloat16 [2, 3072, 768], replicated
- m_w_gate: float32 [2, 768, 3072], P(None, 'dp')
- m_w_up: float32 [2, 768, 3072], P(None, 'dp')
- m_w_down: float32 [2, 3072, 768], P(None, 'dp')
- v_w_gate: float32 [2, 768, 3072], P(None, 'dp')
- v_w_up: float32 [2, 768, 3072], P(None, 'dp')
- v_w_down: float32 [2, 3072, 768], P(None, 'dp')
Outputs:
- output 1: bfloat16 [4, 768, 3072], P('rep'), parts along dimension 0
- output 2: bfloat16 [4, 768, 3072], P('rep'), parts along dimension 0
- output 3: bfloat16 [4, 3072, 768], P('rep'), parts along dimension 0
- output 4: float32 [4, 768, 3072], P('rep', 'dp'), parts along dimension 0
- output 5: float32 [4, 768, 3072], P('rep', 'dp'), parts along dimension 0
- output 6: float32 [4, 3072, 768], P('rep', 'dp'), parts along dimension 0
- output 7: float32 [4, 768, 3072], P('rep', 'dp'), parts along dimension 0
- output 8: float32 [4, 768, 3072], P('rep', 'dp'), parts along dimension 0
- output 9: float32 [4, 3072, 768], P('rep', 'dp'), parts along dimension 0
There are 2 independent parts. A program takes and returns all parts, laid end to end along the dimension named above; an argument that names none is the same for every part.
All inputs are finite; a program needn't handle non-finite values.
Results may differ from a plain program's by a relative error of at most 0.022.
Values are sent between devices in bfloat16 or wider.
A program may use at most 2 GiB of HBM per device.

v0:
```python
import jax
import jax.numpy as jnp
from jax import lax

NAMES = ("w_gate", "w_up", "w_down")


def matmul(a, w):
    return jnp.dot(a, w, preferred_element_type=jnp.float32).astype(jnp.bfloat16)


def normed(h):
    wide = h.astype(jnp.float32)
    scale = lax.rsqrt(jnp.mean(wide**2, -1, keepdims=True) + 1e-6)
    return (wide * scale).astype(jnp.bfloat16)


def layer(h, w):
    a = normed(h)
    gate = jnp.dot(a, w["w_gate"], preferred_element_type=jnp.float32)
    up = jnp.dot(a, w["w_up"], preferred_element_type=jnp.float32)
    return h + matmul((jax.nn.silu(gate) * up).astype(jnp.bfloat16), w["w_down"])


def adamw(w, m, v, g):
    m = 0.9 * m + 0.1 * g
    v = 0.95 * v + 0.05 * g * g
    step = m * lax.rsqrt(v + 1e-8) + 0.1 * w
    return (w - 0.02 * step).astype(jnp.bfloat16), m, v


def stack(weights, h):
    for number in range(weights["w_gate"].shape[0]):
        h = layer(h, {name: w[number] for name, w in weights.items()})
    return h


def solution(mesh):
    groups = mesh.shape["rep"]

    def step(x, dy, *arrays):
        weights, m, v = (arrays[i : i + 3] for i in (0, 3, 6))
        x, dy = (t.reshape(groups, -1, *t.shape[1:]) for t in (x, dy))

        def of_a_group(x, dy):
            _, back = jax.vjp(lambda w: stack(w, x), dict(zip(NAMES, weights, strict=True)))
            by_weights = back(dy)[0]
            gradients = [by_weights[name].astype(jnp.float32) for name in NAMES]
            new = [adamw(w.astype(jnp.float32), m, v, g) for w, m, v, g in zip(weights, m, v, gradients, strict=True)]
            return tuple(one[which] for which in range(3) for one in new)

        return tuple(t.reshape(-1, *t.shape[2:]) for t in jax.vmap(of_a_group)(x, dy))

    return step
```

profile of v0, /device:TPU:0, one launch (start us, length us, event | category | flops | bytes accessed | tf_op | source)
XLA Modules:
  0.0 877.0 jit_solution(1434949176584556349)
XLA Ops:
  12.9 15.9 %fusion.88 = f32[2048,3072]{1,0:T(8,128)} fusion(bf16[2,768,3072]{2,1,0:T(8,128)(2,1)} %param, bf16[1,2048,768]{2,1,0:T(8,128)(2,1)S(1)} %copy-done.1, f32[2048]{0:T(1024)S(1)} %add_rsqrt_fusion), kind=kOutput, calls=%fused_computation.112 | convolution fusion | flops 9668395008 | bytes 33038336 | tf_op jit(solution)/vmap(jvp())/dot_general | solution.py:20
  28.8 15.9 %fusion.86 = f32[2048,3072]{1,0:T(8,128)} fusion(bf16[2,768,3072]{2,1,0:T(8,128)(2,1)} %param.3, bf16[1,2048,768]{2,1,0:T(8,128)(2,1)S(1)} %copy-done.1, f32[2048]{0:T(1024)S(1)} %add_rsqrt_fusion), kind=kOutput, calls=%fused_computation.110 | convolution fusion | flops 9668395008 | bytes 33038336 | tf_op jit(solution)/vmap(jvp())/dot_general | solution.py:21
  44.7 21.8 %fusion.26 = bf16[2048,3072]{1,0:T(8,128)(2,1)} fusion(f32[2048,3072]{1,0:T(8,128)} %fusion.86, f32[2048,3072]{1,0:T(8,128)} %fusion.88), kind=kLoop, calls=%fused_computation.35 | loop fusion | flops 37748736 | bytes 62914560
  66.5 15.0 %fusion.39 = (f32[2048]{0:T(1024)S(1)}, bf16[1,1,2048,768]{2,3,1,0:T(8,128)(2,1)S(1)}) fusion(bf16[2048,3072]{1,0:T(8,128)(2,1)} %fusion.26, bf16[2,3072,768]{2,1,0:T(8,128)(2,1)} %param.4, bf16[1,2048,768]{1,2,0:T(8,128)(2,1)S(1)} %copy-done.4), kind=kOutput, calls=%fused_computation.59 | convolution fusion | flops 9671538688 | bytes 23601152 | tf_op jit(solution)/vmap(jvp())/dot_general | solution.py:9
  82.2 16.0 %fusion.75 = f32[2048,3072]{1,0:T(8,128)} fusion(bf16[2,768,3072]{2,1,0:T(8,128)(2,1)} %param, bf16[1,1,2048,768]{2,3,1,0:T(8,128)(2,1)S(1)} %get-tuple-element.10, f32[2048]{0:T(1024)S(1)} %bitcast.359), kind=kOutput, calls=%fused_computation.99 | convolution fusion | flops 9668395008 | bytes 33038336 | tf_op jit(solution)/vmap(jvp())/dot_general | solution.py:20
  98.3 16.0 %fusion.79 = f32[2048,3072]{1,0:T(8,128)} fusion(bf16[2,768,3072]{2,1,0:T(8,128)(2,1)} %param.3, bf16[1,1,2048,768]{2,3,1,0:T(8,128)(2,1)S(1)} %get-tuple-element.10, f32[2048]{0:T(1024)S(1)} %bitcast.360), kind=kOutput, calls=%fused_computation.103 | convolution fusion | flops 9668395008 | bytes 33038336 | tf_op jit(solution)/vmap(jvp())/dot_general | solution.py:21
  114.3 14.8 %convolution_convert_fusion.1 = bf16[2048,3072]{1,0:T(8,128)(2,1)} fusion(bf16[2,3072,768]{2,1,0:T(8,128)(2,1)} %param.4, bf16[1,2048,768]{2,1,0:T(8,128)(2,1)S(1)} %copy-done.2), kind=kOutput, calls=%fused_computation.44 | convolution fusion | flops 9669967872 | bytes 20447232 | tf_op jit(solution)/vmap(transpose(jvp()))/dot_general | solution.py:9
  132.3 21.1 %fusion.6 = bf16[2048,3072]{1,0:T(8,128)(2,1)S(1)} fusion(f32[2048,3072]{1,0:T(8,128)} %fusion.75, f32[2048,3072]{1,0:T(8,128)} %fusion.79, bf16[2048,3072]{1,0:T(8,128)(2,1)} %convolution_convert_fusion.1), kind=kLoop, calls=%fused_computation.11 | loop fusion | flops 75497472 | bytes 75497472
  170.4 17.5 %fusion.41 = (f32[2048]{0:T(1024)S(1)}, bf16[2048,768]{0,1:T(8,128)(2,1)S(1)}) fusion(bf16[1,1,2048,768]{2,3,1,0:T(8,128)(2,1)S(1)} %copy-done.7, bf16[2048,768]{0,1:T(8,128)(2,1)S(1)} %fusion.102, bf16[2,768,3072]{2,1,0:T(8,128)(2,1)} %param.3, bf16[2048,3072]{1,0:T(8,128)(2,1)} %convolution_convert_fusion.1, f32[2048,3072]{1,0:T(8,128)} %fusion.75), kind=kOutput, calls=%fused_computation.61 | convolution fusion | flops 9710860288 | bytes 51912704 | tf_op jit(solution)/vmap(transpose(jvp()))/dot_general | solution.py:21
  191.9 15.8 %convolution_bitcast_fusion = f32[1,3072,768]{2,1,0:T(8,128)} fusion(bf16[2048,3072]{1,0:T(8,128)(2,1)} %fusion.26, bf16[2048,768]{0,1:T(8,128)(2,1)S(1)} %fusion.113), kind=kOutput, calls=%fused_computation.72 | convolution fusion | flops 9663676416 | bytes 25165824 | tf_op jit(solution)/vmap(transpose(jvp()))/dot_general | solution.py:9
  209.6 23.8 %fusion.42 = f32[1,3072,768]{2,1,0:T(8,128)} fusion(f32[2048,3072]{1,0:T(8,128)} %fusion.79, f32[2048,3072]{1,0:T(8,128)} %fusion.75, bf16[1,2048,768]{2,1,0:T(8,128)(2,1)S(1)} %copy-done.3), kind=kOutput, calls=%fused_computation.74 | convolution fusion | flops 9701425152 | bytes 62914560 | tf_op jit(solution)/vmap(transpose(jvp()))/dot_general | solution.py:9
  233.5 16.0 %convolution_convert_fusion = bf16[2048,3072]{1,0:T(8,128)(2,1)} fusion(bf16[2048,768]{0,1:T(8,128)(2,1)} %copy-done.8, bf16[2,3072,768]{2,1,0:T(8,128)(2,1)} %param.4), kind=kOutput, calls=%fused_computation.43 | convolution fusion | flops 9669967872 | bytes 20447232 | tf_op jit(solution)/vmap(transpose(jvp()))/dot_general | solution.py:9
  249.5 19.1 %fusion.51 = f32[1,768,3072]{2,1,0:T(8,128)} fusion(bf16[2048,3072]{1,0:T(8,128)(2,1)} %convolution_convert_fusion, f32[2048,3072]{1,0:T(8,128)} %fusion.88, bf16[1,2048,768]{1,2,0:T(8,128)(2,1)S(1)} %copy-done.5, f32[2048]{0:T(1024)S(1)} %copy-done.14), kind=kOutput, calls=%fused_computation.77 | convolution fusion | flops 9706143744 | bytes 50339840 | tf_op jit(solution)/vmap(transpose(jvp()))/dot_general | solution.py:21
  269.4 20.3 %fusion.45 = f32[1,768,3072]{2,1,0:T(8,128)} fusion(bf16[2048,3072]{1,0:T(8,128)(2,1)} %convolution_convert_fusion.1, f32[2048,3072]{1,0:T(8,128)} %fusion.75, bf16[1,1,2048,768]{2,3,1,0:T(8,128)(2,1)} %copy-done.6, f32[2048]{0:T(1024)S(1)} %bitcast.362), kind=kOutput, calls=%fused_computation.75 | convolution fusion | flops 9706143744 | bytes 50339840 | tf_op jit(solution)/vmap(transpose(jvp()))/dot_general | solution.py:21
  289.8 16.0 %convolution_bitcast_fusion.1 = f32[1,768,3072]{2,1,0:T(8,128)} fusion(bf16[2048,3072]{1,0:T(8,128)(2,1)} %copy-done, bf16[1,1,2048,768]{2,3,1,0:T(8,128)(2,1)} %copy-done.6, f32[2048]{0:T(1024)S(1)} %bitcast.363), kind=kOutput, calls=%fused_computation.73 | convolution fusion | flops 9668395008 | bytes 25174016 | tf_op jit(solution)/vmap(transpose(jvp()))/dot_general | solution.py:20
  305.8 27.7 %fusion.48 = f32[1,768,3072]{2,1,0:T(8,128)} fusion(f32[2048,3072]{1,0:T(8,128)} %fusion.88, f32[2048,3072]{1,0:T(8,128)} %fusion.86, bf16[2048,3072]{1,0:T(8,128)(2,1)} %convolution_convert_fusion, bf16[1,2048,768]{1,2,0:T(8,128)(2,1)S(1)} %copy-done.5, f32[2048]{0:T(1024)S(1)} %copy-done.14), kind=kOutput, calls=%fused_computation.76 | convolution fusion | flops 9737601024 | bytes 75505664 | tf_op jit(solution)/vmap(transpose(jvp()))/dot_general | solution.py:20
  337.2 19.1 %reduce-scatter.27.cloned.1.call-done = f32[1,768,768]{2,1,0:T(8,128)} async-done(((f32[1,3072,768]{2,1,0:T(8,128)}), f32[1,768,768]{2,1,0:T(8,128)}) %reduce-scatter.27.cloned.1.call-update) | async-done | bytes 2359312
  366.6 64.4 %reduce-scatter.25.cloned.1.call-done = f32[1,192,3072]{2,1,0:T(8,128)} async-done(((f32[1,768,3072]{2,1,0:T(8,128)}), f32[1,192,3072]{2,1,0:T(8,128)}) %reduce-scatter.25.cloned.1.call-update) | async-done | bytes 2359312
  432.9 72.1 %reduce-scatter.23.cloned.1.call-done = f32[1,192,3072]{2,1,0:T(8,128)} async-done(((f32[1,768,3072]{2,1,0:T(8,128)}), f32[1,192,3072]{2,1,0:T(8,128)}) %reduce-scatter.23.cloned.1.call-update) | async-done | bytes 2359312
  515.3 64.2 %reduce-scatter.19.cloned.1.call-done = f32[1,192,3072]{2,1,0:T(8,128)} async-done(((f32[1,768,3072]{2,1,0:T(8,128)}), f32[1,192,3072]{2,1,0:T(8,128)}) %reduce-scatter.19.cloned.1.call-update) | async-done | bytes 2359312
  581.4 72.7 %reduce-scatter.21.cloned.1.call-done = f32[1,192,3072]{2,1,0:T(8,128)} async-done(((f32[1,768,3072]{2,1,0:T(8,128)}), f32[1,192,3072]{2,1,0:T(8,128)}) %reduce-scatter.21.cloned.1.call-update) | async-done | bytes 2359312
  664.7 52.8 %all-gather.14.cloned.1.call-done = bf16[1,2,3072,768]{3,2,1,0:T(8,128)(2,1)} async-done(((bf16[1,2,768,768]{3,2,1,0:T(8,128)(2,1)}), bf16[1,2,3072,768]{3,2,1,0:T(8,128)(2,1)}) %all-gather.14.cloned.1.call-update) | async-done | bytes 9437200 | tf_op jit(solution)/reshape | solution.py:52
  717.5 63.9 %all-gather.12.cloned.1.call-done = bf16[1,2,768,3072]{3,2,1,0:T(8,128)(2,1)} async-done(((bf16[1,2,192,3072]{3,2,1,0:T(8,128)(2,1)}), bf16[1,2,768,3072]{3,2,1,0:T(8,128)(2,1)}) %all-gather.12.cloned.1.call-update) | async-done | bytes 9437200 | tf_op jit(solution)/reshape | solution.py:52
  781.4 63.9 %all-gather.10.cloned.1.call-done = bf16[1,2,768,3072]{3,2,1,0:T(8,128)(2,1)} async-done(((bf16[1,2,192,3072]{3,2,1,0:T(8,128)(2,1)}), bf16[1,2,768,3072]{3,2,1,0:T(8,128)(2,1)}) %all-gather.10.cloned.1.call-update) | async-done | bytes 9437200 | tf_op jit(solution)/reshape | solution.py:52
  (73 shorter events, 95.6 us)
Async XLA Ops:
  7.2 2.8 copy-start.1
  7.2 328.2 %reduce-scatter.29.cloned.1.call-start = ((), (), s32[]{:S(2)}) async-start(), calls=%async_computation.14 | async-start | bytes 11796480
  12.9 15.9 %copy-start.13 = (f32[2048]{0:T(1024)}, f32[2048]{0:T(1024)S(1)}, u32[]{:S(2)}) copy-start(f32[2048]{0:T(1024)S(1)} %add_rsqrt_fusion) | copy-start | bytes 24580
  44.7 21.8 %copy-start.4 = (bf16[1,2048,768]{1,2,0:T(8,128)(2,1)S(1)}, bf16[1,2048,768]{1,2,0:T(8,128)(2,1)}, u32[]{:S(2)}) copy-start(bf16[1,2048,768]{1,2,0:T(8,128)(2,1)} %copy) | copy-start | bytes 9437188
  81.5 16.8 %copy-start.6 = (bf16[1,1,2048,768]{2,3,1,0:T(8,128)(2,1)}, bf16[1,1,2048,768]{2,3,1,0:T(8,128)(2,1)S(1)}, u32[]{:S(2)}) copy-start(bf16[1,1,2048,768]{2,3,1,0:T(8,128)(2,1)S(1)} %get-tuple-element.10) | copy-start | bytes 9437188
  81.5 0.7 copy-start.9
  82.2 105.8 %copy-start.11 = (f32[1,1,2048]{2,1,0:T(1,128)}, f32[1,1,2048]{2,1,0:T(1,128)S(1)}, u32[]{:S(2)}) copy-start(f32[1,1,2048]{2,1,0:T(1,128)S(1)} %rsqrt.31) | copy-start | bytes 24580
  98.3 16.0 %copy-start.2 = (bf16[1,2048,768]{2,1,0:T(8,128)(2,1)S(1)}, bf16[1,2048,768]{2,1,0:T(8,128)(2,1)}, u32[]{:S(2)}) copy-start(bf16[1,2048,768]{2,1,0:T(8,128)(2,1)} %param.5) | copy-start | bytes 9437188
  153.4 4.5 copy-start
  157.9 12.5 %copy-start.7 = (bf16[1,1,2048,768]{2,3,1,0:T(8,128)(2,1)S(1)}, bf16[1,1,2048,768]{2,3,1,0:T(8,128)(2,1)}, u32[]{:S(2)}) copy-start(bf16[1,1,2048,768]{2,3,1,0:T(8,128)(2,1)} %copy-done.6) | copy-start | bytes 9437188
  170.4 17.5 %copy-start.10 = (f32[2048]{0:T(1024)S(1)}, f32[2048]{0:T(1024)}, u32[]{:S(2)}) copy-start(f32[2048]{0:T(1024)} %copy-done.9) | copy-start | bytes 24580
  190.2 1.7 copy-start.8
  207.7 1.9 copy-start.3
  207.7 148.6 %reduce-scatter.27.cloned.1.call-start = ((), (), s32[]{:S(2)}) async-start(), calls=%async_computation.13 | async-start | bytes 11796480
  233.4 16.1 %copy-start.5 = (bf16[1,2048,768]{1,2,0:T(8,128)(2,1)S(1)}, bf16[1,2048,768]{1,2,0:T(8,128)(2,1)}, u32[]{:S(2)}) copy-start(bf16[1,2048,768]{1,2,0:T(8,128)(2,1)} %copy) | copy-start | bytes 9437188
  233.5 16.1 %copy-start.14 = (f32[2048]{0:T(1024)S(1)}, f32[2048]{0:T(1024)}, u32[]{:S(2)}) copy-start(f32[2048]{0:T(1024)} %copy-done.13) | copy-start | bytes 24580
  233.5 197.6 %reduce-scatter.25.cloned.1.call-start = ((), (), s32[]{:S(2)}) async-start(), calls=%async_computation.12 | async-start | bytes 11796480
  268.7 0.7 copy-start.12
  268.7 236.3 %reduce-scatter.23.cloned.1.call-start = ((), (), s32[]{:S(2)}) async-start(), calls=%async_computation.11 | async-start | bytes 11796480
  289.7 289.8 %reduce-scatter.19.cloned.1.call-start = ((), (), s32[]{:S(2)}) async-start(), calls=%async_computation.9 | async-start | bytes 11796480
  305.8 348.3 %reduce-scatter.21.cloned.1.call-start = ((), (), s32[]{:S(2)}) async-start(), calls=%async_computation.10 | async-start | bytes 11796480
  333.5 383.9 %all-gather.14.cloned.1.call-start = ((), (), s32[]{:S(2)}) async-start(), calls=%async_computation.8 | async-start | bytes 11796480 | tf_op jit(solution)/reshape | solution.py:52
  366.6 414.8 %all-gather.12.cloned.1.call-start = ((), (), s32[]{:S(2)}) async-start(), calls=%async_computation.7 | async-start | bytes 11796480 | tf_op jit(solution)/reshape | solution.py:52
  515.3 330.0 %all-gather.10.cloned.1.call-start = ((), (), s32[]{:S(2)}) async-start(), calls=%async_computation.6 | async-start | bytes 11796480 | tf_op jit(solution)/reshape | solution.py:52
  (1 other events, 0.7 us)
Sparse Core Ops, SparseCore 0:
  207.9 74.3 reduce-scatter.28
  284.8 71.5 reduce-scatter.26
  359.5 71.5 reduce-scatter.24
  433.5 71.5 reduce-scatter.22
  508.0 71.5 reduce-scatter.18
  582.5 71.5 reduce-scatter.20
  655.6 61.7 all-gather.13
  719.6 61.7 all-gather.11
  783.5 61.7 all-gather.9
where the time goes:
time: 886 us; the launch traced here: 877 us
  waiting for transfers between devices  473 us (53%)
  matrix products  263 us (30%)
  other arithmetic  84.2 us (10%)
  local copies, waits for them, and re-layouts  41.2 us (5%)
  between operations  15.2 us (2%)
    unnamed x15, waiting for transfers between devices  293 us
    reshape x3, waiting for transfers between devices, step(): t.reshape(-1, *t.shape[2:])  181 us
    dot_general x5, matrix products, layer(): up = jnp.dot(a, w['w_up'], preferred_element_type=jnp.float32)  88.9 us
    dot_general x5, matrix products, layer(): gate = jnp.dot(a, w['w_gate'], preferred_element_type=jnp.float32)  88.2 us
    dot_general x5, matrix products, matmul(): jnp.dot(a, w, preferred_element_type=jnp.float32).astype(jnp.bfloat16)  85.5 us
    unnamed x3, other arithmetic  45.1 us
    unnamed x37, local copies, waits for them, and re-layouts  40.6 us
    reshape x3, other arithmetic, step(): t.reshape(-1, *t.shape[2:])  25.6 us
  transfers between devices with their start and end apart: 9, of which 8 were waited for; matrix products, arithmetic and copies ran while one was open for 18% of the time, Pallas kernels for 0%

commit v1 on v0

v1 whole, which is shorter than its diff:
```python
import jax
import jax.numpy as jnp
from jax import lax
from jax.sharding import PartitionSpec as P

NAMES = ("w_gate", "w_up", "w_down")
SIBLING = [(i, i ^ 1) for i in range(4)]
CROSS = [(i, i ^ 2) for i in range(4)]
BF, F32 = jnp.bfloat16, jnp.float32


def dot(a, b, dims, out=BF):
    return lax.dot_general(a, b, (dims, ((), ())), preferred_element_type=F32).astype(out)


def normed(h):
    wide = h.astype(F32)
    scale = lax.rsqrt(jnp.mean(wide**2, -1, keepdims=True) + 1e-6)
    return (wide * scale).astype(BF)


def adamw(w, m, v, g):
    m = 0.9 * m + 0.1 * g
    v = 0.95 * v + 0.05 * g * g
    step = m * lax.rsqrt(v + 1e-8) + 0.1 * w
    return (w - 0.02 * step).astype(BF), m, v


def gated(gate, up):
    return (jax.nn.silu(gate) * up).astype(BF)


def solution(mesh):
    def body(x, dy, wg, wu, wd, mg, mu, md, vg, vu, vd):
        x, dy = x[0], dy[0]
        dp = lax.axis_index("dp")
        side, core = dp // 2, dp % 2
        ws, ms, vs = (wg, wu, wd), (mg, mu, md), (vg, vu, vd)

        def reduce(g):
            rows, cols = g.shape
            g = g.reshape(2, 2, rows // 4, cols)
            mine = lax.dynamic_index_in_dim(g, core, 1, keepdims=False)
            out = lax.dynamic_index_in_dim(g, 1 - core, 1, keepdims=False)
            got = lax.ppermute(out, "dp", SIBLING)
            both = mine.astype(F32) + got.astype(F32)
            own = lax.dynamic_index_in_dim(both, side, 0, keepdims=False)
            send = lax.dynamic_index_in_dim(both, 1 - side, 0, keepdims=False).astype(BF)
            return own + lax.ppermute(send, "dp", CROSS).astype(F32)

        new = {}

        def update(layer, i, g):
            g = reduce(g).astype(BF).astype(F32)
            rows = g.shape[0]
            w = lax.dynamic_slice_in_dim(ws[i][layer], dp * rows, rows, 0).astype(F32)
            nw, nm, nv = adamw(w, ms[i][layer], vs[i][layer], g)
            far = lax.ppermute(nw, "dp", CROSS)
            near = lax.ppermute(nw, "dp", SIBLING)
            diagonal = lax.ppermute(far, "dp", SIBLING)
            new[layer, i] = (nw, near, far, diagonal), nm, nv

        h = [x]
        saved = []
        for n in range(2):
            a = normed(h[n])
            gate = dot(a, wg[n], ((1,), (0,)), F32)
            up = dot(a, wu[n], ((1,), (0,)), F32)
            act = gated(gate, up)
            saved.append((a, gate, up, act))
            if n == 0:
                h.append(h[0] + dot(act, wd[0], ((1,), (0,))))
        d = dy
        for n in (1, 0):
            a, gate, up, act = saved[n]
            update(n, 2, dot(act, d, ((0,), (0,))))
            dact = dot(d, wd[n], ((1,), (1,)))
            dgate, dup = jax.vjp(gated, gate, up)[1](dact)
            dgate, dup = dgate.astype(BF), dup.astype(BF)
            update(n, 0, dot(a, dgate, ((0,), (0,))))
            update(n, 1, dot(a, dup, ((0,), (0,))))
            if n:
                da = dot(dgate, wg[n], ((1,), (1,))) + dot(dup, wu[n], ((1,), (1,)))
                d = d + jax.vjp(normed, h[n])[1](da)[0]

        outs_w = []
        for i in range(3):
            layers = []
            for n in range(2):
                nw, near, far, diagonal = new[n, i][0]
                stacked = jnp.zeros((4, *nw.shape), BF)
                for piece, who in ((nw, dp), (near, dp ^ 1), (far, dp ^ 2), (diagonal, dp ^ 3)):
                    stacked = lax.dynamic_update_index_in_dim(stacked, piece, who, 0)
                layers.append(stacked.reshape(-1, nw.shape[1]))
            outs_w.append(jnp.stack(layers))
        outs_m = [jnp.stack([new[n, i][1] for n in range(2)]) for i in range(3)]
        outs_v = [jnp.stack([new[n, i][2] for n in range(2)]) for i in range(3)]
        return (*outs_w, *outs_m, *outs_v)

    batch, whole, rows = P(("rep", "dp")), P(), P(None, "dp")
    return jax.shard_map(
        body,
        mesh=mesh,
        in_specs=(batch, batch, *(whole,) * 3, *(rows,) * 6),
        out_specs=(*(P("rep"),) * 3, *(P("rep", "dp"),) * 6),
        check_vma=False,
    )
```

time: 886 us -> 693 us (0.78)
  waiting for transfers between devices: 473 us -> 174 us
  local copies, waits for them, and re-layouts: 41.2 us -> 98.7 us
  other arithmetic: 84.2 us -> 115 us
  starting transfers between devices: 0.37 us -> 21.8 us
  between operations: 15.2 us -> 2.01 us
  matrix products: 263 us -> 272 us
    unnamed x15 -> x0, waiting for transfers between devices: 293 us -> none
    reshape x3 -> x0, waiting for transfers between devices: 181 us -> none  [step(): t.reshape(-1, *t.shape[2:])]
    ppermute x0 -> x30, waiting for transfers between devices: none -> 174 us  [the longest x6 104 us: update(): far = lax.ppermute(nw, 'dp', CROSS)]
    another operation x0 -> x15, other arithmetic: none -> 68.7 us  [the longest x6 29 us: body(): outs_v = [jnp.stack([new[n, i][2] for n in range(2)]) for i in range(3)]]
    unnamed x3 -> x15, other arithmetic: 45.1 us -> 0.01 us
    reshape x3 -> x0, other arithmetic: 25.6 us -> none  [step(): t.reshape(-1, *t.shape[2:])]
    slice x0 -> x3, local copies, waits for them, and re-layouts: none -> 24.9 us  [the longest x1 8.55 us: body(): up = dot(a, wu[n], ((1,), (0,)), F32)]
    dynamic_update_slice x0 -> x6, other arithmetic: none -> 24.4 us  [body(): stacked = lax.dynamic_update_index_in_dim(stacked, piece, who, 0)]
  transfers between devices with their start and end apart: 9 -> 30, of which waited for: 8 -> 9; matrix products, arithmetic and copies ran while one was open for 18% -> 48% of each run, Pallas kernels for 0% -> 0%
where the time goes in v1:
time: 693 us; the launch traced here: 684 us
  matrix products  272 us (39%)
  waiting for transfers between devices  174 us (25%)
  other arithmetic  115 us (17%)
  local copies, waits for them, and re-layouts  98.7 us (14%)
  starting transfers between devices  21.8 us (3%)
    dot_general x15, matrix products, dot(): lax.dot_general(a, b, (dims, ((), ())), preferred_element_type=F32)  272 us
    ppermute x6, waiting for transfers between devices, update(): far = lax.ppermute(nw, 'dp', CROSS)  104 us
    ppermute x6, waiting for transfers between devices, reduce(): return own + lax.ppermute(send, 'dp', CROSS).astype(F32)  68.5 us
    unnamed x166, local copies, waits for them, and re-layouts  33 us
    another operation x6, other arithmetic, body(): outs_v = [jnp.stack([new[n, i][2] for n in range(2)]) for i in range(3)]  29 us
    another operation x3, other arithmetic, body(): outs_w.append(jnp.stack(layers))  25.1 us
    dynamic_update_slice x6, other arithmetic, body(): stacked = lax.dynamic_update_index_in_dim(stacked, piece, who, 0)  24.4 us
    add x6, other arithmetic, reduce(): both = mine.astype(F32) + got.astype(F32)  18.7 us
  transfers between devices with their start and end apart: 30, of which 9 were waited for; matrix products, arithmetic and copies ran while one was open for 48% of the time, Pallas kernels for 0%

profile of v1, /device:TPU:0, one launch (start us, length us, event | category | flops | bytes accessed | tf_op | source)
XLA Modules:
  0.0 683.7 jit_solution(11528632399088915586)
XLA Ops:
  6.9 16.0 %fusion.42 = f32[2048,3072]{1,0:T(8,128)} fusion(bf16[1,2048,768]{2,1,0:T(8,128)(2,1)S(1)} %copy-done.35, f32[2048]{0:T(1024)S(1)} %add_rsqrt_fusion, bf16[2,768,3072]{2,1,0:T(8,128)(2,1)} %param.13), kind=kOutput, calls=%fused_computation.74 | convolution fusion | flops 9668395008 | bytes 33038336 | tf_op jit(solution)/shard_map/dot_general | solution.py:13
  22.9 27.8 %multiply_convert_fusion.1 = (bf16[2048,3072]{1,0:T(8,128)(2,1)}, f32[2048,3072]{1,0:T(8,128)}) fusion(f32[2048,3072]{1,0:T(8,128)} %fusion.42, bf16[2,768,3072]{2,1,0:T(8,128)(2,1)} %param.14, bf16[1,2048,768]{2,1,0:T(8,128)(2,1)} %param.11, f32[2048]{0:T(1024)S(1)} %add_rsqrt_fusion), kind=kOutput, calls=%fused_computation.17 | convolution fusion | flops 9706143744 | bytes 70787072 | tf_op jit(solution)/shard_map/dot_general | solution.py:13
  50.7 14.9 %fusion.19 = (f32[2048]{0:T(1024)S(1)}, bf16[2048,768]{0,1:T(8,128)(2,1)S(1)}) fusion(bf16[2048,3072]{1,0:T(8,128)(2,1)} %get-tuple-element.53, bf16[2,3072,768]{2,1,0:T(8,128)(2,1)} %param.15, bf16[1,2048,768]{1,2,0:T(8,128)(2,1)S(1)} %copy.20), kind=kOutput, calls=%fused_computation.39 | convolution fusion | flops 9671538688 | bytes 23601152 | tf_op jit(solution)/shard_map/dot_general | solution.py:13
  65.6 16.8 %fusion.35 = f32[2048,3072]{1,0:T(8,128)} fusion(bf16[2048,768]{0,1:T(8,128)(2,1)S(1)} %get-tuple-element.56, f32[2048]{0:T(1024)S(1)} %fusion.127, bf16[2,768,3072]{2,1,0:T(8,128)(2,1)} %param.14), kind=kOutput, calls=%fused_computation.67 | convolution fusion | flops 9668395008 | bytes 33038336 | tf_op jit(solution)/shard_map/dot_general | solution.py:13
  82.5 15.9 %fusion.31 = f32[2048,3072]{1,0:T(8,128)} fusion(bf16[2048,768]{0,1:T(8,128)(2,1)S(1)} %get-tuple-element.56, f32[2048]{0:T(1024)S(1)} %fusion.127, bf16[2,768,3072]{2,1,0:T(8,128)(2,1)} %param.13), kind=kOutput, calls=%fused_computation.63 | convolution fusion | flops 9668395008 | bytes 33038336 | tf_op jit(solution)/shard_map/dot_general | solution.py:13
  98.4 20.1 %fusion.28 = bf16[3072,768]{1,0:T(8,128)(2,1)S(1)} fusion(f32[2048,3072]{1,0:T(8,128)} %fusion.35, f32[2048,3072]{1,0:T(8,128)} %fusion.31, bf16[1,2048,768]{2,1,0:T(8,128)(2,1)S(1)} %copy-done.36), kind=kOutput, calls=%fused_computation.45 | convolution fusion | flops 9703784448 | bytes 58195968 | tf_op jit(solution)/shard_map/dot_general | solution.py:13
  123.1 31.1 %fusion = (bf16[2048,3072]{1,0:T(8,128)(2,1)}, bf16[2048,3072]{1,0:T(8,128)(2,1)}) fusion(f32[2048,3072]{1,0:T(8,128)} %fusion.31, f32[2048,3072]{1,0:T(8,128)} %fusion.35, bf16[2,3072,768]{2,1,0:T(8,128)(2,1)} %param.15, bf16[1,2048,768]{2,1,0:T(8,128)(2,1)S(1)} %copy-done.36), kind=kOutput, calls=%fused_computation.6 | convolution fusion | flops 9764339712 | bytes 83361792 | tf_op jit(solution)/shard_map/dot_general | solution.py:13
  157.5 14.5 %fusion.50 = bf16[2048,768]{0,1:T(8,128)(2,1)S(1)} fusion(bf16[2048,3072]{1,0:T(8,128)(2,1)} %get-tuple-element.33, bf16[2,768,3072]{2,1,0:T(8,128)(2,1)} %param.14), kind=kOutput, calls=%fused_computation.84 | convolution fusion | flops 9665249280 | bytes 20447232 | tf_op jit(solution)/shard_map/dot_general | solution.py:13
  172.0 14.9 %fusion.21 = (f32[2048]{0:T(1024)S(1)}, bf16[2048,768]{0,1:T(8,128)(2,1)S(1)}) fusion(bf16[2048,768]{0,1:T(8,128)(2,1)S(1)} %copy-done.38, bf16[2048,768]{0,1:T(8,128)(2,1)S(1)} %fusion.50, bf16[2048,3072]{1,0:T(8,128)(2,1)} %get-tuple-element.34, bf16[2,768,3072]{2,1,0:T(8,128)(2,1)} %param.13), kind=kOutput, calls=%fused_computation.41 | convolution fusion | flops 9673111552 | bytes 26746880 | tf_op jit(solution)/shard_map/dot_general | solution.py:13
  189.2 14.3 %convolution_convert_fusion.2 = bf16[3072,768]{1,0:T(8,128)(2,1)S(1)} fusion(bf16[2048,3072]{1,0:T(8,128)(2,1)} %get-tuple-element.53, bf16[2048,768]{0,1:T(8,128)(2,1)S(1)} %fusion.57), kind=kOutput, calls=%fused_computation.46 | convolution fusion | flops 9666035712 | bytes 20447232 | tf_op jit(solution)/shard_map/dot_general | solution.py:13
  207.1 13.5 %convolution_convert_fusion.3 = bf16[768,3072]{1,0:T(8,128)(2,1)S(1)} fusion(bf16[2048,3072]{1,0:T(8,128)(2,1)} %get-tuple-element.33, bf16[2048,768]{0,1:T(8,128)(2,1)S(1)} %copy-done.38, f32[2048]{0:T(1024)S(1)} %copy-done.46), kind=kOutput, calls=%fused_computation.47 | convolution fusion | flops 9670754304 | bytes 20455424 | tf_op jit(solution)/shard_map/dot_general | solution.py:13
  225.0 14.8 %convolution_convert_fusion = bf16[2048,3072]{1,0:T(8,128)(2,1)} fusion(bf16[2048,768]{0,1:T(8,128)(2,1)} %copy-done.40, bf16[2,3072,768]{2,1,0:T(8,128)(2,1)S(1)} %bitcast.372), kind=kOutput, calls=%fused_computation.23 | convolution fusion | flops 9669967872 | bytes 20447232 | tf_op jit(solution)/shard_map/dot_general | solution.py:13
  239.9 18.8 %fusion.25 = bf16[768,3072]{1,0:T(8,128)(2,1)} fusion(bf16[2048,3072]{1,0:T(8,128)(2,1)} %convolution_convert_fusion, f32[2048,3072]{1,0:T(8,128)} %fusion.42, bf16[1,2048,768]{1,2,0:T(8,128)(2,1)S(1)} %copy-done.13, f32[2048]{0:T(1024)S(1)} %copy-done.50), kind=kOutput, calls=%fused_computation.44 | convolution fusion | flops 9714794496 | bytes 45621248 | tf_op jit(solution)/shard_map/dot_general | solution.py:13
  262.1 12.9 %convolution_convert_fusion.4 = bf16[768,3072]{1,0:T(8,128)(2,1)S(1)} fusion(bf16[2048,3072]{1,0:T(8,128)(2,1)} %get-tuple-element.34, bf16[2048,768]{0,1:T(8,128)(2,1)S(1)} %copy-done.39, f32[2048]{0:T(1024)S(1)} %copy-done.46), kind=kOutput, calls=%fused_computation.48 | convolution fusion | flops 9670754304 | bytes 20455424 | tf_op jit(solution)/shard_map/dot_general | solution.py:13
  287.2 25.9 %fusion.22 = bf16[768,3072]{1,0:T(8,128)(2,1)} fusion(f32[2048,3072]{1,0:T(8,128)} %fusion.42, f32[2048,3072]{1,0:T(8,128)} %get-tuple-element.54, bf16[2048,3072]{1,0:T(8,128)(2,1)} %convolution_convert_fusion, bf16[1,2048,768]{1,2,0:T(8,128)(2,1)S(1)} %copy-done.13, f32[2048]{0:T(1024)S(1)} %copy-done.50), kind=kOutput, calls=%fused_computation.43 | convolution fusion | flops 9746251776 | bytes 70787072 | tf_op jit(solution)/shard_map/dot_general | solution.py:13
  313.1 8.6 %fusion.153 = (bf16[1,768,3072]{2,1,0:T(8,128)(2,1)}, bf16[1,768,3072]{2,1,0:T(8,128)(2,1)}) fusion(bf16[2,768,3072]{2,1,0:T(8,128)(2,1)} %param.14), kind=kLoop, calls=%fused_computation.223 | loop fusion | bytes 18874368 | tf_op jit(solution)/shard_map/slice | solution.py:68
  367.9 23.1 %collective-permute-done.21 = bf16[768,768]{1,0:T(8,128)(2,1)} collective-permute-done((bf16[768,768]{1,0:T(8,128)(2,1)}, bf16[768,768]{1,0:T(8,128)(2,1)}, u32[]{:S(2)}, u32[]{:S(2)}) %collective-permute-start.21) | collective-permute-done | bytes 1179680 | tf_op jit(solution)/shard_map/ppermute | solution.py:49
  406.6 9.7 %collective-permute-done.16 = bf16[192,3072]{1,0:T(8,128)(2,1)} collective-permute-done((bf16[192,3072]{1,0:T(8,128)(2,1)}, bf16[192,3072]{1,0:T(8,128)(2,1)}, u32[]{:S(2)}, u32[]{:S(2)}) %collective-permute-start.16) | collective-permute-done | bytes 1179680 | tf_op jit(solution)/shard_map/ppermute | solution.py:49
  418.3 23.3 %collective-permute-done.11 = bf16[192,3072]{1,0:T(8,128)(2,1)} collective-permute-done((bf16[192,3072]{1,0:T(8,128)(2,1)}, bf16[192,3072]{1,0:T(8,128)(2,1)}, u32[]{:S(2)}, u32[]{:S(2)}) %collective-permute-start.11) | collective-permute-done | bytes 1179680 | tf_op jit(solution)/shard_map/ppermute | solution.py:49
  479.6 12.5 %collective-permute-done.1 = bf16[192,3072]{1,0:T(8,128)(2,1)} collective-permute-done((bf16[192,3072]{1,0:T(8,128)(2,1)}, bf16[192,3072]{1,0:T(8,128)(2,1)}, u32[]{:S(2)}, u32[]{:S(2)}) %collective-permute-start.1) | collective-permute-done | bytes 1179680 | tf_op jit(solution)/shard_map/ppermute | solution.py:49
  530.7 11.9 %collective-permute-done.13 = bf16[192,3072]{1,0:T(8,128)(2,1)} collective-permute-done((bf16[192,3072]{1,0:T(8,128)(2,1)}, bf16[192,3072]{1,0:T(8,128)(2,1)}, u32[]{:S(2)}, u32[]{:S(2)}) %collective-permute-start.13) | collective-permute-done | bytes 1179680 | tf_op jit(solution)/shard_map/ppermute | solution.py:58
  546.1 21.9 %collective-permute-done.18 = bf16[192,3072]{1,0:T(8,128)(2,1)S(1)} collective-permute-done((bf16[192,3072]{1,0:T(8,128)(2,1)}, bf16[192,3072]{1,0:T(8,128)(2,1)S(1)}, u32[]{:S(2)}, u32[]{:S(2)}) %collective-permute-start.18) | collective-permute-done | bytes 1179680 | tf_op jit(solution)/shard_map/ppermute | solution.py:58
  568.7 23.8 %collective-permute-done.3 = bf16[192,3072]{1,0:T(8,128)(2,1)S(1)} collective-permute-done((bf16[192,3072]{1,0:T(8,128)(2,1)S(1)}, bf16[192,3072]{1,0:T(8,128)(2,1)S(1)}, u32[]{:S(2)}, u32[]{:S(2)}) %collective-permute-start.3) | collective-permute-done | bytes 1179680 | tf_op jit(solution)/shard_map/ppermute | solution.py:58
  598.8 46.3 %collective-permute-done.8 = bf16[192,3072]{1,0:T(8,128)(2,1)S(1)} collective-permute-done((bf16[192,3072]{1,0:T(8,128)(2,1)S(1)}, bf16[192,3072]{1,0:T(8,128)(2,1)S(1)}, u32[]{:S(2)}, u32[]{:S(2)}) %collective-permute-start.8) | collective-permute-done | bytes 1179680 | tf_op jit(solution)/shard_map/ppermute | solution.py:58
  (303 shorter events, 228.6 us)
Async XLA Ops:
  122.3 209.4 %collective-permute-start.25 = (bf16[2,768,768]{2,1,0:T(8,128)(2,1)}, bf16[2,768,768]{2,1,0:T(8,128)(2,1)}, u32[]{:S(2)}, u32[]{:S(2)}) collective-permute-start(bf16[2,768,768]{2,1,0:T(8,128)(2,1)} %dynamic-slice_bitcast_fusion), channel_id=1, source_target_pairs={{0,1},{1,0},{2,3},{3,2},{4,5},{5,4},{6,7},{7,6}} | collective-permute-start | bytes 7077896 | tf_op jit(solution)/shard_map/ppermute | solution.py:45
  207.0 128.8 %collective-permute-start.20 = (bf16[2,768,768]{2,1,0:T(8,128)(2,1)}, bf16[2,768,768]{2,1,0:T(8,128)(2,1)}, u32[]{:S(2)}, u32[]{:S(2)}) collective-permute-start(bf16[2,768,768]{2,1,0:T(8,128)(2,1)} %dynamic-slice_bitcast_fusion.1), channel_id=1, source_target_pairs={{0,1},{1,0},{2,3},{3,2},{4,5},{5,4},{6,7},{7,6}} | collective-permute-start | bytes 7077896 | tf_op jit(solution)/shard_map/ppermute | solution.py:45
  224.4 118.7 %collective-permute-start.15 = (bf16[2,192,3072]{2,1,0:T(8,128)(2,1)}, bf16[2,192,3072]{2,1,0:T(8,128)(2,1)}, u32[]{:S(2)}, u32[]{:S(2)}) collective-permute-start(bf16[2,192,3072]{2,1,0:T(8,128)(2,1)} %dynamic-slice_bitcast_fusion.2), channel_id=1, source_target_pairs={{0,1},{1,0},{2,3},{3,2},{4,5},{5,4},{6,7},{7,6}} | collective-permute-start | bytes 7077896 | tf_op jit(solution)/shard_map/ppermute | solution.py:45
  262.1 85.0 %collective-permute-start.10 = (bf16[2,192,3072]{2,1,0:T(8,128)(2,1)}, bf16[2,192,3072]{2,1,0:T(8,128)(2,1)}, u32[]{:S(2)}, u32[]{:S(2)}) collective-permute-start(bf16[2,192,3072]{2,1,0:T(8,128)(2,1)} %dynamic-slice_bitcast_fusion.3), channel_id=1, source_target_pairs={{0,1},{1,0},{2,3},{3,2},{4,5},{5,4},{6,7},{7,6}} | collective-permute-start | bytes 7077896 | tf_op jit(solution)/shard_map/ppermute | solution.py:45
  278.7 74.2 %collective-permute-start.5 = (bf16[2,192,3072]{2,1,0:T(8,128)(2,1)}, bf16[2,192,3072]{2,1,0:T(8,128)(2,1)}, u32[]{:S(2)}, u32[]{:S(2)}) collective-permute-start(bf16[2,192,3072]{2,1,0:T(8,128)(2,1)} %dynamic-slice_bitcast_fusion.4), channel_id=1, source_target_pairs={{0,1},{1,0},{2,3},{3,2},{4,5},{5,4},{6,7},{7,6}} | collective-permute-start | bytes 7077896 | tf_op jit(solution)/shard_map/ppermute | solution.py:45
  335.9 31.2 %collective-permute-start.26 = (bf16[768,768]{1,0:T(8,128)(2,1)}, bf16[768,768]{1,0:T(8,128)(2,1)}, u32[]{:S(2)}, u32[]{:S(2)}) collective-permute-start(bf16[768,768]{1,0:T(8,128)(2,1)} %fusion.120), channel_id=1, source_target_pairs={{0,2},{1,3},{2,0},{3,1},{4,6},{5,7},{6,4},{7,5}} | collective-permute-start | bytes 3538952 | tf_op jit(solution)/shard_map/ppermute | solution.py:49
  343.1 47.9 %collective-permute-start.21 = (bf16[768,768]{1,0:T(8,128)(2,1)}, bf16[768,768]{1,0:T(8,128)(2,1)}, u32[]{:S(2)}, u32[]{:S(2)}) collective-permute-start(bf16[768,768]{1,0:T(8,128)(2,1)} %fusion.119), channel_id=1, source_target_pairs={{0,2},{1,3},{2,0},{3,1},{4,6},{5,7},{6,4},{7,5}} | collective-permute-start | bytes 3538952 | tf_op jit(solution)/shard_map/ppermute | solution.py:49
  347.1 69.1 %collective-permute-start.16 = (bf16[192,3072]{1,0:T(8,128)(2,1)}, bf16[192,3072]{1,0:T(8,128)(2,1)}, u32[]{:S(2)}, u32[]{:S(2)}) collective-permute-start(bf16[192,3072]{1,0:T(8,128)(2,1)} %fusion.118), channel_id=1, source_target_pairs={{0,2},{1,3},{2,0},{3,1},{4,6},{5,7},{6,4},{7,5}} | collective-permute-start | bytes 3538952 | tf_op jit(solution)/shard_map/ppermute | solution.py:49
  352.9 88.7 %collective-permute-start.11 = (bf16[192,3072]{1,0:T(8,128)(2,1)}, bf16[192,3072]{1,0:T(8,128)(2,1)}, u32[]{:S(2)}, u32[]{:S(2)}) collective-permute-start(bf16[192,3072]{1,0:T(8,128)(2,1)} %fusion.117), channel_id=1, source_target_pairs={{0,2},{1,3},{2,0},{3,1},{4,6},{5,7},{6,4},{7,5}} | collective-permute-start | bytes 3538952 | tf_op jit(solution)/shard_map/ppermute | solution.py:49
  360.3 117.3 %collective-permute-start.6 = (bf16[192,3072]{1,0:T(8,128)(2,1)}, bf16[192,3072]{1,0:T(8,128)(2,1)}, u32[]{:S(2)}, u32[]{:S(2)}) collective-permute-start(bf16[192,3072]{1,0:T(8,128)(2,1)} %fusion.116), channel_id=1, source_target_pairs={{0,2},{1,3},{2,0},{3,1},{4,6},{5,7},{6,4},{7,5}} | collective-permute-start | bytes 3538952 | tf_op jit(solution)/shard_map/ppermute | solution.py:49
  367.1 125.0 %collective-permute-start.1 = (bf16[192,3072]{1,0:T(8,128)(2,1)}, bf16[192,3072]{1,0:T(8,128)(2,1)}, u32[]{:S(2)}, u32[]{:S(2)}) collective-permute-start(bf16[192,3072]{1,0:T(8,128)(2,1)} %fusion.115), channel_id=1, source_target_pairs={{0,2},{1,3},{2,0},{3,1},{4,6},{5,7},{6,4},{7,5}} | collective-permute-start | bytes 3538952 | tf_op jit(solution)/shard_map/ppermute | solution.py:49
  401.2 193.7 %collective-permute-start.22 = (bf16[768,768]{1,0:T(8,128)(2,1)}, bf16[768,768]{1,0:T(8,128)(2,1)}, u32[]{:S(2)}, u32[]{:S(2)}) collective-permute-start(bf16[768,768]{1,0:T(8,128)(2,1)} %get-tuple-element.22), channel_id=1, source_target_pairs={{0,1},{1,0},{2,3},{3,2},{4,5},{5,4},{6,7},{7,6}} | collective-permute-start | bytes 3538952 | tf_op jit(solution)/shard_map/ppermute | solution.py:59
  416.2 178.7 %collective-permute-start.23 = (bf16[768,768]{1,0:T(8,128)(2,1)}, bf16[768,768]{1,0:T(8,128)(2,1)}, u32[]{:S(2)}, u32[]{:S(2)}) collective-permute-start(bf16[768,768]{1,0:T(8,128)(2,1)} %get-tuple-element.22), channel_id=1, source_target_pairs={{0,2},{1,3},{2,0},{3,1},{4,6},{5,7},{6,4},{7,5}} | collective-permute-start | bytes 3538952 | tf_op jit(solution)/shard_map/ppermute | solution.py:58
  456.0 69.3 %collective-permute-start.12 = (bf16[192,3072]{1,0:T(8,128)(2,1)}, bf16[192,3072]{1,0:T(8,128)(2,1)}, u32[]{:S(2)}, u32[]{:S(2)}) collective-permute-start(bf16[192,3072]{1,0:T(8,128)(2,1)} %get-tuple-element.26), channel_id=1, source_target_pairs={{0,1},{1,0},{2,3},{3,2},{4,5},{5,4},{6,7},{7,6}} | collective-permute-start | bytes 3538952 | tf_op jit(solution)/shard_map/ppermute | solution.py:59
  477.6 65.0 %collective-permute-start.13 = (bf16[192,3072]{1,0:T(8,128)(2,1)}, bf16[192,3072]{1,0:T(8,128)(2,1)}, u32[]{:S(2)}, u32[]{:S(2)}) collective-permute-start(bf16[192,3072]{1,0:T(8,128)(2,1)} %get-tuple-element.26), channel_id=1, source_target_pairs={{0,2},{1,3},{2,0},{3,1},{4,6},{5,7},{6,4},{7,5}} | collective-permute-start | bytes 3538952 | tf_op jit(solution)/shard_map/ppermute | solution.py:58
  492.1 36.8 %collective-permute-start.17 = (bf16[192,3072]{1,0:T(8,128)(2,1)}, bf16[192,3072]{1,0:T(8,128)(2,1)}, u32[]{:S(2)}, u32[]{:S(2)}) collective-permute-start(bf16[192,3072]{1,0:T(8,128)(2,1)} %get-tuple-element.28), channel_id=1, source_target_pairs={{0,1},{1,0},{2,3},{3,2},{4,5},{5,4},{6,7},{7,6}} | collective-permute-start | bytes 3538952 | tf_op jit(solution)/shard_map/ppermute | solution.py:59
  525.4 42.6 %collective-permute-start.18 = (bf16[192,3072]{1,0:T(8,128)(2,1)}, bf16[192,3072]{1,0:T(8,128)(2,1)S(1)}, u32[]{:S(2)}, u32[]{:S(2)}) collective-permute-start(bf16[192,3072]{1,0:T(8,128)(2,1)} %get-tuple-element.28), channel_id=1, source_target_pairs={{0,2},{1,3},{2,0},{3,1},{4,6},{5,7},{6,4},{7,5}} | collective-permute-start | bytes 3538952 | tf_op jit(solution)/shard_map/ppermute | solution.py:58
  528.9 39.1 %collective-permute-start.2 = (bf16[192,3072]{1,0:T(8,128)(2,1)S(1)}, bf16[192,3072]{1,0:T(8,128)(2,1)S(1)}, u32[]{:S(2)}, u32[]{:S(2)}) collective-permute-start(bf16[192,3072]{1,0:T(8,128)(2,1)S(1)} %copy-done.44), channel_id=1, source_target_pairs={{0,1},{1,0},{2,3},{3,2},{4,5},{5,4},{6,7},{7,6}} | collective-permute-start | bytes 3538952 | tf_op jit(solution)/shard_map/ppermute | solution.py:59
  542.6 49.9 %collective-permute-start.3 = (bf16[192,3072]{1,0:T(8,128)(2,1)S(1)}, bf16[192,3072]{1,0:T(8,128)(2,1)S(1)}, u32[]{:S(2)}, u32[]{:S(2)}) collective-permute-start(bf16[192,3072]{1,0:T(8,128)(2,1)S(1)} %copy-done.44), channel_id=1, source_target_pairs={{0,2},{1,3},{2,0},{3,1},{4,6},{5,7},{6,4},{7,5}} | collective-permute-start | bytes 3538952 | tf_op jit(solution)/shard_map/ppermute | solution.py:58
  567.9 77.3 %collective-permute-start.27 = (bf16[768,768]{1,0:T(8,128)(2,1)S(1)}, bf16[768,768]{1,0:T(8,128)(2,1)S(1)}, u32[]{:S(2)}, u32[]{:S(2)}) collective-permute-start(bf16[768,768]{1,0:T(8,128)(2,1)S(1)} %copy-done.42), channel_id=1, source_target_pairs={{0,1},{1,0},{2,3},{3,2},{4,5},{5,4},{6,7},{7,6}} | collective-permute-start | bytes 3538952 | tf_op jit(solution)/shard_map/ppermute | solution.py:59
  592.5 53.3 %collective-permute-start.28 = (bf16[768,768]{1,0:T(8,128)(2,1)S(1)}, bf16[768,768]{1,0:T(8,128)(2,1)S(1)}, u32[]{:S(2)}, u32[]{:S(2)}) collective-permute-start(bf16[768,768]{1,0:T(8,128)(2,1)S(1)} %copy-done.42), channel_id=1, source_target_pairs={{0,2},{1,3},{2,0},{3,1},{4,6},{5,7},{6,4},{7,5}} | collective-permute-start | bytes 3538952 | tf_op jit(solution)/shard_map/ppermute | solution.py:58
  594.4 50.7 %collective-permute-start.8 = (bf16[192,3072]{1,0:T(8,128)(2,1)S(1)}, bf16[192,3072]{1,0:T(8,128)(2,1)S(1)}, u32[]{:S(2)}, u32[]{:S(2)}) collective-permute-start(bf16[192,3072]{1,0:T(8,128)(2,1)S(1)} %copy-done.43), channel_id=1, source_target_pairs={{0,2},{1,3},{2,0},{3,1},{4,6},{5,7},{6,4},{7,5}} | collective-permute-start | bytes 3538952 | tf_op jit(solution)/shard_map/ppermute | solution.py:58
  594.9 53.6 %collective-permute-start.14 = (bf16[192,3072]{1,0:T(8,128)(2,1)}, bf16[192,3072]{1,0:T(8,128)(2,1)S(1)}, u32[]{:S(2)}, u32[]{:S(2)}) collective-permute-start(bf16[192,3072]{1,0:T(8,128)(2,1)} %collective-permute-done.13), channel_id=1, source_target_pairs={{0,1},{1,0},{2,3},{3,2},{4,5},{5,4},{6,7},{7,6}} | collective-permute-start | bytes 3538952 | tf_op jit(solution)/shard_map/ppermute | solution.py:60
  594.9 54.2 %collective-permute-start.24 = (bf16[768,768]{1,0:T(8,128)(2,1)}, bf16[768,768]{1,0:T(8,128)(2,1)S(1)}, u32[]{:S(2)}, u32[]{:S(2)}) collective-permute-start(bf16[768,768]{1,0:T(8,128)(2,1)} %collective-permute-done.23), channel_id=1, source_target_pairs={{0,1},{1,0},{2,3},{3,2},{4,5},{5,4},{6,7},{7,6}} | collective-permute-start | bytes 3538952 | tf_op jit(solution)/shard_map/ppermute | solution.py:60
  (88 other events, 1159.8 us)

commit v2 on v0

v2 whole, which is shorter than its diff:
```python
import functools

import jax
import jax.numpy as jnp
from jax import lax
from jax.experimental import pallas as pl
from jax.experimental.pallas import tpu as pltpu
from jax.sharding import PartitionSpec as P


SIBLING = [(i, i ^ 1) for i in range(4)]
CROSS = [(i, i ^ 2) for i in range(4)]
BF, F32 = jnp.bfloat16, jnp.float32
T, D, FF, N = 2048, 768, 3072, 4
TILE = FF // N

def mm(a, b, ca=1, cb=0):
    return lax.dot_general(a, b, (((ca,), (cb,)), ((), ())), preferred_element_type=F32)

def norm(h):
    wide = h.astype(F32)
    return (wide * lax.rsqrt(jnp.mean(wide * wide, -1, keepdims=True) + 1e-6)).astype(BF)

def params(mib=63, n=1):
    return pltpu.CompilerParams(dimension_semantics=("arbitrary",) * n, vmem_limit_bytes=mib * 2**20)

def cost(mms):
    return pl.CostEstimate(flops=int(mms * 2 * T * D * FF), bytes_accessed=int(2e7), transcendentals=0)

def once(shape, index):
    return pl.BlockSpec(shape, index, pipeline_mode=pl.Buffered(1))

def fwd_body(x_ref, wg_ref, wu_ref, wd_ref, g_ref, u_ref, a_ref, h_ref, b_ref):
    x = x_ref[...]
    a = norm(x)
    a_ref[...] = a
    acc = None
    for f in range(N):
        at = slice(f * TILE, (f + 1) * TILE)
        g = mm(a, wg_ref[0, :, at])
        u = mm(a, wu_ref[0, :, at])
        g_ref[:, at] = g
        u_ref[:, at] = u
        act = (g * jax.nn.sigmoid(g) * u).astype(BF)
        p = mm(act, wd_ref[0, at, :])
        acc = p if acc is None else acc + p
    h = x + acc.astype(BF)
    h_ref[...] = h
    b_ref[...] = norm(h)

def fwd(x, wg, wu, wd, mb=512):
    row = lambda c: pl.BlockSpec((mb, c), lambda m: (m, 0))
    sds = jax.ShapeDtypeStruct
    return pl.pallas_call(fwd_body, grid=(T // mb,),
        in_specs=[row(D), once((1, D, FF), lambda m: (0, 0, 0)), once((1, D, FF), lambda m: (0, 0, 0)), once((1, FF, D), lambda m: (0, 0, 0))],
        out_specs=[row(FF), row(FF), row(D), row(D), row(D)],
        out_shape=[sds((T, FF), F32), sds((T, FF), F32), sds((T, D), BF), sds((T, D), BF), sds((T, D), BF)],
        compiler_params=params(), cost_estimate=cost(3), name="fwd")(x, wg, wu, wd)

def gate_bwd(g, u, dact):
    s = jax.nn.sigmoid(g)
    silu = g * s
    d = dact.astype(BF).astype(F32)
    dup = (d * silu).astype(BF)
    dgate = (d * u * (s + silu * (1.0 - s))).astype(BF)
    return silu, dgate, dup

def back_body(recompute, q_ref, d_ref, a_ref, *refs):
    if recompute:
        wg_ref, wu_ref, wd_ref, act_ref, dg_ref, du_ref, keep_ref, send_ref, accg, accu = refs
    else:
        g_ref, u_ref, wd_ref, act_ref, keep_ref, send_ref, accg, accu = refs
    m = pl.program_id(0)
    a = a_ref[...]
    if recompute:
        g = mm(a, wg_ref[0])
        u = mm(a, wu_ref[0])
    else:
        g, u = g_ref[...], u_ref[...]
    dact = mm(d_ref[...], wd_ref[0], 1, 1)
    silu, dgate, dup = gate_bwd(g, u, dact)
    act_ref[...] = (silu * u).astype(BF)
    if recompute:
        dg_ref[...] = dgate
        du_ref[...] = dup
    pg = mm(a, dgate, 0, 0)
    pu = mm(a, dup, 0, 0)

    @pl.when(m == 0)
    def _():
        accg[...] = pg
        accu[...] = pu

    @pl.when(m > 0)
    def _():
        accg[...] += pg
        accu[...] += pu

    @pl.when(m == pl.num_programs(0) - 1)
    def _():
        core = q_ref[0] % 2
        rows = D // 4
        for side in range(2):
            mine = pl.ds(pl.multiple_of((2 * side + core) * rows, 64), rows)
            other = pl.ds(pl.multiple_of((2 * side + 1 - core) * rows, 64), rows)
            for i, acc in enumerate((accg, accu)):
                keep_ref[side, i] = acc[mine, :]
                send_ref[side, i] = acc[other, :].astype(BF)

def back(layer, t, q, d, a, first, second, wd, mb=512):
    sds = jax.ShapeDtypeStruct
    recompute = layer == 1
    row = lambda c: pl.BlockSpec((mb, c), lambda m, q: (m, 0))
    col = pl.BlockSpec((mb, TILE), lambda m, q: (m, t))
    wcol = once((1, D, TILE), lambda m, q: (layer, 0, t))
    wrow = once((1, TILE, D), lambda m, q: (layer, t, 0))
    extra = ([wcol, wcol] if recompute else [col, col]) + [wrow]
    whole = lambda *s: pl.BlockSpec(s, lambda m, q: (0,) * len(s))
    tile = sds((T, TILE), BF)
    outs = [tile] * (3 if recompute else 1)
    return pl.pallas_call(functools.partial(back_body, recompute),
        grid_spec=pltpu.PrefetchScalarGridSpec(num_scalar_prefetch=1, grid=(T // mb,),
            in_specs=[row(D), row(D), *extra],
            out_specs=[row(TILE)] * len(outs) + [whole(2, 2, D // 4, TILE)] * 2,
            scratch_shapes=[pltpu.VMEM((D, TILE), F32)] * 2),
        out_shape=[*outs, sds((2, 2, D // 4, TILE), F32), sds((2, 2, D // 4, TILE), BF)],
        compiler_params=params(), cost_estimate=cost(1.25 if recompute else 0.75))(q, d, a, first, second, wd)

def down_body(q_ref, a0, a1, a2, a3, d_ref, keep_ref, send_ref, acc):
    m = pl.program_id(0)
    d = d_ref[...]
    for t, a in enumerate((a0, a1, a2, a3)):
        p = mm(a[...], d, 0, 0)

        @pl.when(m == 0)
        def _():
            acc[t] = p

        @pl.when(m > 0)
        def _():
            acc[t] += p

    @pl.when(m == pl.num_programs(0) - 1)
    def _():
        core = q_ref[0] % 2
        for side in range(2):
            keep_ref[side] = acc[2 * side + core]
            send_ref[side] = acc[2 * side + 1 - core].astype(BF)

def down(q, acts, d, mb=512):
    sds = jax.ShapeDtypeStruct
    row = lambda c: pl.BlockSpec((mb, c), lambda m, q: (m, 0))
    whole = lambda *s: pl.BlockSpec(s, lambda m, q: (0,) * len(s))
    return pl.pallas_call(down_body,
        grid_spec=pltpu.PrefetchScalarGridSpec(num_scalar_prefetch=1, grid=(T // mb,),
            in_specs=[row(TILE)] * 4 + [row(D)], out_specs=[whole(2, TILE, D)] * 2,
            scratch_shapes=[pltpu.VMEM((4, TILE, D), F32)]),
        out_shape=[sds((2, TILE, D), F32), sds((2, TILE, D), BF)],
        compiler_params=params(), cost_estimate=cost(1), name="down")(q, *acts, d)

def input_body(dy_ref, h_ref, *refs):
    dgs, dus, (wg_ref, wu_ref, o_ref) = refs[:4], refs[4:8], refs[8:]
    da = None
    for ds, w in ((dgs, wg_ref), (dus, wu_ref)):
        s = None
        for t in range(4):
            p = mm(ds[t][...], w[0, :, t * TILE:(t + 1) * TILE], 1, 1)
            s = p if s is None else s + p
        s = s.astype(BF)
        da = s if da is None else da + s
    da = da.astype(F32)
    wide = h_ref[...].astype(F32)
    scale = lax.rsqrt(jnp.mean(wide * wide, -1, keepdims=True) + 1e-6)
    along = jnp.sum(da * wide, -1, keepdims=True)
    dh = da * scale - wide * (along * scale * scale * scale * (1.0 / D))
    o_ref[...] = dy_ref[...] + dh.astype(BF)

def input_grad(dy, h, dgs, dus, wg, wu, mb=512):
    row = lambda c: pl.BlockSpec((mb, c), lambda m: (m, 0))
    w = once((1, D, FF), lambda m: (1, 0, 0))
    return pl.pallas_call(input_body, grid=(T // mb,),
        in_specs=[row(D), row(D)] + [row(TILE)] * 8 + [w, w], out_specs=row(D),
        out_shape=jax.ShapeDtypeStruct((T, D), BF),
        compiler_params=params(), cost_estimate=cost(2), name="input_grad")(dy, h, *dgs, *dus, wg, wu)


def adamw(w, m, v, g):
    m = 0.9 * m + 0.1 * g
    v = 0.95 * v + 0.05 * g * g
    step = m * lax.rsqrt(v + 1e-8) + 0.1 * w
    return (w - 0.02 * step).astype(BF), m, v


def update_body(pairs, q_ref, keep_ref, near_ref, got_ref, *refs):
    ins, outs = refs[: 3 * pairs], refs[-(3 * pairs + 1) :]
    for i in range(pairs):
        w, m, v = ins[3 * i : 3 * i + 3]
        g = (keep_ref[0, i] + near_ref[0, i].astype(F32) + got_ref[i].astype(F32)).astype(BF).astype(F32)
        nw, nm, nv = adamw(w[0].astype(F32), m[0], v[0], g)
        outs[3 * i][0] = nw
        outs[3 * i + 1][0] = nm
        outs[3 * i + 2][0] = nv
        outs[-1][i] = nw


def update(layer, t, q, keep, near, got, arrays, chain):
    pairs = len(arrays) // 3
    sds = jax.ShapeDtypeStruct
    if pairs == 2:
        rows, width, steps = D // 4, TILE, 3
        part = width // steps
        mine = pl.BlockSpec((1, rows, part), lambda i, q: (layer, q[0], t * steps + i))
        state = pl.BlockSpec((1, rows, part), lambda i, q: (layer, 0, t * steps + i))
        kept = pl.BlockSpec((1, pairs, rows, part), lambda i, q: (q[0] // 2, 0, 0, i))
        flat = pl.BlockSpec((pairs, rows, part), lambda i, q: (0, 0, i))
    else:
        rows, width, steps = TILE, D, 4
        part = rows // steps
        mine = pl.BlockSpec((1, part, width), lambda i, q: (layer, q[0] * steps + i, 0))
        state = pl.BlockSpec((1, part, width), lambda i, q: (layer, i, 0))
        kept = pl.BlockSpec((1, pairs, part, width), lambda i, q: (q[0] // 2, 0, i, 0))
        flat = pl.BlockSpec((pairs, part, width), lambda i, q: (0, i, 0))
    specs = [mine, state, state] * pairs
    shapes = [sds(a.shape, a.dtype) for a in arrays]
    anys = [pl.BlockSpec(memory_space=pl.ANY)] * len(chain)
    alias = {4 + 3 * pairs + i: i for i in range(len(chain))}
    out = pl.pallas_call(
        functools.partial(update_body, pairs),
        grid_spec=pltpu.PrefetchScalarGridSpec(
            num_scalar_prefetch=1, grid=(steps,), in_specs=[kept, kept, flat, *specs, *anys], out_specs=[*specs, flat]
        ),
        out_shape=[*shapes, sds((pairs, rows, width), BF)],
        input_output_aliases=alias,
        compiler_params=params(),
        cost_estimate=pl.CostEstimate(flops=10**8, bytes_accessed=8 * 10**6, transcendentals=0),
        name="update",
    )(q, keep, near, got, *arrays, *chain)
    return list(out[:-1]), out[-1]


def place_body(pairs, q_ref, near_ref, far_ref, diagonal_ref, *refs):
    outs = refs[-pairs:]
    step = pl.program_id(0)
    for k, piece in enumerate((near_ref, far_ref, diagonal_ref)):

        @pl.when(step == k)
        def _():
            for i in range(pairs):
                outs[i][0] = piece[i]


def place(layer, t, q, near, far, diagonal, chain):
    pairs = len(chain)
    rows, width = near.shape[1:]
    whole = pl.BlockSpec((pairs, rows, width), lambda i, q: (0, 0, 0))
    spec = pl.BlockSpec((1, rows, width), lambda i, q: (layer, q[0] ^ (i + 1), t))
    return list(
        pl.pallas_call(
            functools.partial(place_body, pairs),
            grid_spec=pltpu.PrefetchScalarGridSpec(
                num_scalar_prefetch=1,
                grid=(3,),
                in_specs=[whole] * 3 + [pl.BlockSpec(memory_space=pl.ANY)] * pairs,
                out_specs=[spec] * pairs,
            ),
            out_shape=[jax.ShapeDtypeStruct(a.shape, a.dtype) for a in chain],
            input_output_aliases={4 + i: i for i in range(pairs)},
            compiler_params=params(),
            cost_estimate=pl.CostEstimate(flops=10**7, bytes_accessed=7 * 10**6, transcendentals=0),
            name="place",
        )(q, near, far, diagonal, *chain)
    )


def after(x, *deps):
    return lax.optimization_barrier((x, *deps))[0]


def sum_body(q_ref, keep_ref, got_ref, o_ref):
    o_ref[...] = (keep_ref[0] + got_ref[0].astype(F32)).astype(BF)


def sum_far(q, keep, got):
    shape = keep.shape[1:]
    part = (*shape[:-1], shape[-1] // 3)
    spec = pl.BlockSpec((1, *part), lambda i, q: (1 - q[0] // 2, 0, 0, i))
    return pl.pallas_call(
        sum_body,
        grid_spec=pltpu.PrefetchScalarGridSpec(
            num_scalar_prefetch=1, grid=(3,), in_specs=[spec, spec], out_specs=pl.BlockSpec(part, lambda i, q: (0, 0, i))
        ),
        out_shape=jax.ShapeDtypeStruct(shape, BF),
        compiler_params=params(),
        cost_estimate=pl.CostEstimate(flops=10**7, bytes_accessed=4 * 10**6, transcendentals=0),
        name="sum_far",
    )(q, keep, got)


def solution(mesh):
    def body(x, dy, wg, wu, wd, mg, mu, md, vg, vu, vd):
        x, dy = x[0], dy[0]
        q = lax.axis_index("dp").reshape(1)
        gate_up, downs = (wg, mg, vg, wu, mu, vu), (wd, md, vd)
        last = [None]
        chains = {2: [], 1: []}

        def run(f, first, *args):
            if last[0] is not None:
                first = after(first, *last[0])
            out = f(first, *args)
            last[0] = [jax.tree.leaves(out)[-1]]
            return out

        def send(x, pairs):
            return lax.ppermute(x, "dp", pairs)

        class Chunk:
            def __init__(self, layer, t, keep, out):
                self.layer, self.t, self.keep = layer, t, keep
                self.pairs = keep.shape[1]
                self.got = send(out, SIBLING)

            def cross(self):
                far = run(lambda keep: sum_far(q, keep, self.got), self.keep)
                self.far = send(far, CROSS)

            def update(self):
                arrays = gate_up if self.pairs == 2 else downs
                chain = chains[self.pairs]
                chain, w = run(lambda keep: update(self.layer, self.t, q, keep, self.got, self.far, arrays, chain), self.keep)
                chains[self.pairs] = chain
                self.wfar = send(w, CROSS)
                self.wnear = send(w, SIBLING)

            def forward(self):
                self.wdiag = send(self.wfar, SIBLING)

            def place(self):
                chain = chains[self.pairs]
                at = list(range(0, 3 * self.pairs, 3))
                placed = run(lambda near: place(self.layer, self.t, q, near, self.wfar, self.wdiag, [chain[i] for i in at]), self.wnear)
                for i, p in zip(at, placed):
                    chain[i] = p

        g0, u0, a0, h1, a1 = run(lambda x: fwd(x, wg, wu, wd), x)
        c, outs = [], []

        def back1(t):
            act, dg, du, keep, out = run(lambda a: back(1, t, q, dy, a, wg, wu, wd), a1)
            outs.append((act, dg, du))
            c.append(Chunk(1, t, keep, out))

        def down_of(layer, acts, d):
            keep, out = run(lambda d: down(q, acts, d), d)
            c.append(Chunk(layer, 0, keep[:, None], out[:, None]))

        back1(0)
        c[0].cross()
        back1(1)
        c[1].cross()
        c[0].update()
        back1(2)
        c[2].cross()
        c[1].update()
        back1(3)
        c[0].forward()
        c[3].cross()
        c[2].update()
        down_of(1, [o[0] for o in outs], dy)
        c[1].forward()
        c[0].place()
        d = run(lambda h: input_grad(dy, h, [o[1] for o in outs], [o[2] for o in outs], wg, wu), h1)
        c[4].cross()
        c[3].update()
        c[2].forward()
        c[1].place()
        acts = []
        for t in range(4):
            act, keep, out = run(lambda d: back(0, t, q, d, a0, g0, u0, wd), d)
            acts.append(act)
            c.append(Chunk(0, t, keep, out))
            if t:
                c[4 + t].cross()
            if t == 0:
                c[2].place()
                c[3].forward()
            if t == 1:
                c[4].update()
            if t == 2:
                c[3].place()
            if t == 3:
                c[5].update()
        down_of(0, acts, d)
        c[8].cross()
        c[4].forward()
        c[6].update()
        c[9].cross()
        c[5].forward()
        c[4].place()
        c[7].update()
        c[6].forward()
        c[5].place()
        c[8].update()
        c[7].forward()
        c[6].place()
        c[9].update()
        c[8].forward()
        c[7].place()
        c[8].place()
        c[9].forward()
        c[9].place()
        g, o = chains[2], chains[1]
        return g[0], g[3], o[0], g[1], g[4], o[1], g[2], g[5], o[2]

    batch, whole, rows = P(("rep", "dp")), P(), P(None, "dp")

    step = jax.shard_map(
        body,
        mesh=mesh,
        in_specs=(batch, batch, *(whole,) * 3, *(rows,) * 6),
        out_specs=(*(P("rep"),) * 3, *(P("rep", "dp"),) * 6),
        check_vma=False,
    )
    shape = lambda dtype, *s: jax.ShapeDtypeStruct(s, dtype)
    tokens = shape(BF, mesh.size, T, D)
    weights = [shape(BF, 2, D, FF)] * 2 + [shape(BF, 2, FF, D)]
    states = [shape(F32, *w.shape) for w in weights]
    jax.eval_shape(step, tokens, tokens, *weights, *states, *states)
    return step
```

time: 886 us -> 644 us (0.73)
  Pallas kernels: 0 us -> 398 us
  waiting for transfers between devices: 473 us -> 205 us
  matrix products: 263 us -> 0 us
  other arithmetic: 84.2 us -> 0 us
  local copies, waits for them, and re-layouts: 41.2 us -> 4.19 us
  starting transfers between devices: 0.37 us -> 26.2 us
  between operations: 15.2 us -> 1.35 us
    pallas_call x0 -> x42, Pallas kernels: none -> 398 us  [the longest x8 152 us: back(): pl.pallas_call(functools.partial(back_body, recompute), grid_spec=pltpu.P...]
    unnamed x15 -> x0, waiting for transfers between devices: 293 us -> none
    dot_general x15 -> x0, matrix products: 263 us -> none  [the longest x5 88.9 us: layer(): up = jnp.dot(a, w['w_up'], preferred_element_type=jnp.float32)]
    ppermute x0 -> x50, waiting for transfers between devices: none -> 205 us  [send(): return lax.ppermute(x, 'dp', pairs)]
    reshape x3 -> x0, waiting for transfers between devices: 181 us -> none  [step(): t.reshape(-1, *t.shape[2:])]
    unnamed x3 -> x0, other arithmetic: 45.1 us -> none
    unnamed x37 -> x22, local copies, waits for them, and re-layouts: 40.6 us -> 4.19 us
    ppermute x0 -> x50, starting transfers between devices: none -> 26.2 us  [send(): return lax.ppermute(x, 'dp', pairs)]
  transfers between devices with their start and end apart: 9 -> 50, of which waited for: 8 -> 17; matrix products, arithmetic and copies ran while one was open for 18% -> 0% of each run, Pallas kernels for 0% -> 34%
where the time goes in v2:
time: 644 us; the launch traced here: 635 us
  Pallas kernels  398 us (62%)
  waiting for transfers between devices  205 us (32%)
  starting transfers between devices  26.2 us (4%)
    ppermute x50, waiting for transfers between devices, send(): return lax.ppermute(x, 'dp', pairs)  205 us
    pallas_call x8, Pallas kernels, back(): pl.pallas_call(functools.partial(back_body, recompute), grid_spec=pltpu.P...  152 us
    pallas_call x10, Pallas kernels, update(): pl.pallas_call(functools.partial(update_body, pairs), grid_spec=pltpu.Pre...  57.6 us
    pallas_call x2, Pallas kernels, down(): pl.pallas_call(down_body, grid_spec=pltpu.PrefetchScalarGridSpec(num_scal...  50.2 us
    pallas_call x1, Pallas kernels, fwd(): pl.pallas_call(fwd_body, grid=(T // mb,), in_specs=[row(D), once((1, D, F...  43.1 us
    pallas_call x10, Pallas kernels, place(): pl.pallas_call(functools.partial(place_body, pairs), grid_spec=pltpu.Pref...  33.7 us
    pallas_call x10, Pallas kernels, sum_far(): pl.pallas_call(sum_body, grid_spec=pltpu.PrefetchScalarGridSpec(num_scala...  32.1 us
    pallas_call x1, Pallas kernels, input_grad(): pl.pallas_call(input_body, grid=(T // mb,), in_specs=[row(D), row(D)] + [...  29.6 us
  transfers between devices with their start and end apart: 50, of which 17 were waited for; matrix products, arithmetic and copies ran while one was open for 0% of the time, Pallas kernels for 34%

profile of v2, /device:TPU:0, one launch (start us, length us, event | category | flops | bytes accessed | tf_op | source)
XLA Modules:
  0.0 634.8 jit_solution(17592262766107702586)
XLA Ops:
  0.6 43.1 %fwd.1 = (f32[2048,3072]{1,0:T(8,128)}, f32[2048,3072]{1,0:T(8,128)}, bf16[2048,768]{1,0:T(8,128)(2,1)}, bf16[2048,768]{1,0:T(8,128)(2,1)}, bf16[2048,768]{1,0:T(8,128)(2,1)}) custom-call(bf16[2048,768]{1,0:T(8,128)(2,1)} %bitcast.11, bf16[2,768,3072]{2,1,0:T(8,128)(2,1)} %refs_0_.26, bf16[2,768,3072]{2,1,0:T(8,128)(2,1)} %refs_3_.15, ...), custom_call_target="tpu_custom_call" | custom-call | flops 28991029248 | bytes 20000000 | tf_op jit(solution)/shard_map/fwd/pallas_call | solution.py:54
  43.8 21.5 %shard_map.178 = (bf16[2048,768]{1,0:T(8,128)(2,1)}, bf16[2048,768]{1,0:T(8,128)(2,1)}, bf16[2048,768]{1,0:T(8,128)(2,1)}, f32[2,2,192,768]{3,2,1,0:T(8,128)}, bf16[2,2,192,768]{3,2,1,0:T(8,128)(2,1)}) custom-call(s32[1]{0:T(128)} %bitcast.q_ref, bf16[2048,768]{1,0:T(8,128)(2,1)} %bitcast.12, bf16[2048,768]{1,0:T(8,128)(2,1)} %get-tuple-element.198.a_ref, ...), custom_call_target="tpu_custom_call" | custom-call | flops 12079595520 | bytes 20000000 | tf_op jit(solution)/shard_map/pallas_call | solution.py:121
  72.0 21.7 %shard_map.179 = (bf16[2048,768]{1,0:T(8,128)(2,1)}, bf16[2048,768]{1,0:T(8,128)(2,1)}, bf16[2048,768]{1,0:T(8,128)(2,1)}, f32[2,2,192,768]{3,2,1,0:T(8,128)}, bf16[2,2,192,768]{3,2,1,0:T(8,128)(2,1)}) custom-call(s32[1]{0:T(128)} %bitcast.q_ref, bf16[2048,768]{1,0:T(8,128)(2,1)} %bitcast.13, bf16[2048,768]{1,0:T(8,128)(2,1)} %get-tuple-element.198.a_ref, ...), custom_call_target="tpu_custom_call" | custom-call | flops 12079595520 | bytes 20000000 | tf_op jit(solution)/shard_map/pallas_call | solution.py:121
  100.1 10.7 %collective-permute-done.2.got_ref = bf16[2,192,768]{2,1,0:T(8,128)(2,1)} collective-permute-done((bf16[2,192,768]{2,1,0:T(8,128)(2,1)S(1)}, bf16[2,192,768]{2,1,0:T(8,128)(2,1)}, u32[]{:S(2)}, u32[]{:S(2)}) %collective-permute-start.2) | collective-permute-done | bytes 589856 | tf_op jit(solution)/shard_map/ppermute | solution.py:315
  116.0 21.5 %shard_map.180 = (bf16[2048,768]{1,0:T(8,128)(2,1)}, bf16[2048,768]{1,0:T(8,128)(2,1)}, bf16[2048,768]{1,0:T(8,128)(2,1)}, f32[2,2,192,768]{3,2,1,0:T(8,128)}, bf16[2,2,192,768]{3,2,1,0:T(8,128)(2,1)}) custom-call(s32[1]{0:T(128)} %bitcast.q_ref, bf16[2048,768]{1,0:T(8,128)(2,1)} %bitcast.14, bf16[2048,768]{1,0:T(8,128)(2,1)} %get-tuple-element.198.a_ref, ...), custom_call_target="tpu_custom_call" | custom-call | flops 12079595520 | bytes 20000000 | tf_op jit(solution)/shard_map/pallas_call | solution.py:121
  143.8 9.7 %collective-permute-done.5.got_ref = bf16[2,192,768]{2,1,0:T(8,128)(2,1)S(1)} collective-permute-done((bf16[2,192,768]{2,1,0:T(8,128)(2,1)}, bf16[2,192,768]{2,1,0:T(8,128)(2,1)S(1)}, u32[]{:S(2)}, u32[]{:S(2)}) %collective-permute-start.5) | collective-permute-done | bytes 589856 | tf_op jit(solution)/shard_map/ppermute | solution.py:315
  159.6 22.0 %shard_map.181 = (bf16[2048,768]{1,0:T(8,128)(2,1)}, bf16[2048,768]{1,0:T(8,128)(2,1)}, bf16[2048,768]{1,0:T(8,128)(2,1)}, f32[2,2,192,768]{3,2,1,0:T(8,128)}, bf16[2,2,192,768]{3,2,1,0:T(8,128)(2,1)}) custom-call(s32[1]{0:T(128)} %bitcast.q_ref, bf16[2048,768]{1,0:T(8,128)(2,1)} %bitcast.15, bf16[2048,768]{1,0:T(8,128)(2,1)} %get-tuple-element.198.a_ref, ...), custom_call_target="tpu_custom_call" | custom-call | flops 12079595520 | bytes 20000000 | tf_op jit(solution)/shard_map/pallas_call | solution.py:121
  183.6 14.5 %collective-permute-done.8.far_ref = bf16[2,192,768]{2,1,0:T(8,128)(2,1)} collective-permute-done((bf16[2,192,768]{2,1,0:T(8,128)(2,1)}, bf16[2,192,768]{2,1,0:T(8,128)(2,1)}, u32[]{:S(2)}, u32[]{:S(2)}) %collective-permute-start.8) | collective-permute-done | bytes 589856 | tf_op jit(solution)/shard_map/ppermute | solution.py:315
  216.8 25.0 %down.2 = (f32[2,768,768]{2,1,0:T(8,128)}, bf16[2,768,768]{2,1,0:T(8,128)(2,1)}) custom-call(s32[1]{0:T(128)} %bitcast.q_ref, bf16[2048,768]{1,0:T(8,128)(2,1)} %get-tuple-element.183.a0, bf16[2048,768]{1,0:T(8,128)(2,1)} %get-tuple-element.184.a1, bf16[2048,768]{1,0:T(8,128)(2,1)} %get-tuple-element.186.a2, bf16[2048,768]{1,0:T(8,128)(2,1)} %get-tuple-element.199.a3, ...), custom_call_target="tpu_custom_call" | custom-call | flops 9663676416 | bytes 20000000 | tf_op jit(solution)/shard_map/down/pallas_call | solution.py:154
  247.5 29.6 %input_grad.1.d_ref = bf16[2048,768]{1,0:T(8,128)(2,1)} custom-call(bf16[2048,768]{1,0:T(8,128)(2,1)} %bitcast.17, bf16[2048,768]{1,0:T(8,128)(2,1)} %get-tuple-element.217.h_ref, bf16[2048,768]{1,0:T(8,128)(2,1)} %get-tuple-element.218.refs_0_, bf16[2048,768]{1,0:T(8,128)(2,1)} %get-tuple-element.219.refs_1_, bf16[2048,768]{1,0:T(8,128)(2,1)} %get-tuple-element.220.refs_2_, ...), custom_call_target="tpu_custom_call" | custom-call | flops 19327352832 | bytes 20000000 | tf_op jit(solution)/shard_map/input_grad/pallas_call | solution.py:181
  290.7 16.5 %shard_map.182 = (bf16[2048,768]{1,0:T(8,128)(2,1)}, f32[2,2,192,768]{3,2,1,0:T(8,128)}, bf16[2,2,192,768]{3,2,1,0:T(8,128)(2,1)}) custom-call(s32[1]{0:T(128)} %bitcast.q_ref, bf16[2048,768]{1,0:T(8,128)(2,1)} %input_grad.1.d_ref, bf16[2048,768]{1,0:T(8,128)(2,1)} %get-tuple-element.240.a_ref, f32[2048,3072]{1,0:T(8,128)} %get-tuple-element.241.refs_0_, ...), custom_call_target="tpu_custom_call" | custom-call | flops 7247757312 | bytes 20000000 | tf_op jit(solution)/shard_map/pallas_call | solution.py:121
  312.6 16.2 %shard_map.183 = (bf16[2048,768]{1,0:T(8,128)(2,1)}, f32[2,2,192,768]{3,2,1,0:T(8,128)}, bf16[2,2,192,768]{3,2,1,0:T(8,128)(2,1)}) custom-call(s32[1]{0:T(128)} %bitcast.q_ref, bf16[2048,768]{1,0:T(8,128)(2,1)} %input_grad.1.d_ref, bf16[2048,768]{1,0:T(8,128)(2,1)} %get-tuple-element.240.a_ref, f32[2048,3072]{1,0:T(8,128)} %get-tuple-element.241.refs_0_, ...), custom_call_target="tpu_custom_call" | custom-call | flops 7247757312 | bytes 20000000 | tf_op jit(solution)/shard_map/pallas_call | solution.py:121
  328.9 19.6 %collective-permute-done.22.far_ref = bf16[2,192,768]{2,1,0:T(8,128)(2,1)} collective-permute-done((bf16[2,192,768]{2,1,0:T(8,128)(2,1)}, bf16[2,192,768]{2,1,0:T(8,128)(2,1)}, u32[]{:S(2)}, u32[]{:S(2)}) %collective-permute-start.22) | collective-permute-done | bytes 589856 | tf_op jit(solution)/shard_map/ppermute | solution.py:315
  359.4 16.3 %shard_map.184 = (bf16[2048,768]{1,0:T(8,128)(2,1)}, f32[2,2,192,768]{3,2,1,0:T(8,128)}, bf16[2,2,192,768]{3,2,1,0:T(8,128)(2,1)}) custom-call(s32[1]{0:T(128)} %bitcast.q_ref, bf16[2048,768]{1,0:T(8,128)(2,1)} %input_grad.1.d_ref, bf16[2048,768]{1,0:T(8,128)(2,1)} %get-tuple-element.240.a_ref, f32[2048,3072]{1,0:T(8,128)} %get-tuple-element.241.refs_0_, ...), custom_call_target="tpu_custom_call" | custom-call | flops 7247757312 | bytes 20000000 | tf_op jit(solution)/shard_map/pallas_call | solution.py:121
  384.2 16.3 %shard_map.185 = (bf16[2048,768]{1,0:T(8,128)(2,1)}, f32[2,2,192,768]{3,2,1,0:T(8,128)}, bf16[2,2,192,768]{3,2,1,0:T(8,128)(2,1)}) custom-call(s32[1]{0:T(128)} %bitcast.q_ref, bf16[2048,768]{1,0:T(8,128)(2,1)} %input_grad.1.d_ref, bf16[2048,768]{1,0:T(8,128)(2,1)} %get-tuple-element.240.a_ref, f32[2048,3072]{1,0:T(8,128)} %get-tuple-element.241.refs_0_, ...), custom_call_target="tpu_custom_call" | custom-call | flops 7247757312 | bytes 20000000 | tf_op jit(solution)/shard_map/pallas_call | solution.py:121
  409.7 25.2 %down.3 = (f32[2,768,768]{2,1,0:T(8,128)}, bf16[2,768,768]{2,1,0:T(8,128)(2,1)}) custom-call(s32[1]{0:T(128)} %bitcast.q_ref, bf16[2048,768]{1,0:T(8,128)(2,1)} %get-tuple-element.272.a0, bf16[2048,768]{1,0:T(8,128)(2,1)} %get-tuple-element.273.a1, bf16[2048,768]{1,0:T(8,128)(2,1)} %get-tuple-element.274.a2, bf16[2048,768]{1,0:T(8,128)(2,1)} %get-tuple-element.275.a3, ...), custom_call_target="tpu_custom_call" | custom-call | flops 9663676416 | bytes 20000000 | tf_op jit(solution)/shard_map/down/pallas_call | solution.py:154
  437.5 26.6 %collective-permute-done.31.far_ref = bf16[1,768,768]{2,1,0:T(8,128)(2,1)} collective-permute-done((bf16[1,768,768]{2,1,0:T(8,128)(2,1)}, bf16[1,768,768]{2,1,0:T(8,128)(2,1)}, u32[]{:S(2)}, u32[]{:S(2)}) %collective-permute-start.31) | collective-permute-done | bytes 1179680 | tf_op jit(solution)/shard_map/ppermute | solution.py:315
  464.1 12.2 %collective-permute-done.29.got_ref = bf16[2,192,768]{2,1,0:T(8,128)(2,1)} collective-permute-done((bf16[2,192,768]{2,1,0:T(8,128)(2,1)S(1)}, bf16[2,192,768]{2,1,0:T(8,128)(2,1)}, u32[]{:S(2)}, u32[]{:S(2)}) %collective-permute-start.29) | collective-permute-done | bytes 589856 | tf_op jit(solution)/shard_map/ppermute | solution.py:315
  493.0 12.5 %collective-permute-done.34.far_ref = bf16[2,192,768]{2,1,0:T(8,128)(2,1)} collective-permute-done((bf16[2,192,768]{2,1,0:T(8,128)(2,1)}, bf16[2,192,768]{2,1,0:T(8,128)(2,1)}, u32[]{:S(2)}, u32[]{:S(2)}) %collective-permute-start.34) | collective-permute-done | bytes 589856 | tf_op jit(solution)/shard_map/ppermute | solution.py:315
  505.7 12.3 %collective-permute-done.40.far_ref = bf16[2,192,768]{2,1,0:T(8,128)(2,1)} collective-permute-done((bf16[2,192,768]{2,1,0:T(8,128)(2,1)}, bf16[2,192,768]{2,1,0:T(8,128)(2,1)}, u32[]{:S(2)}, u32[]{:S(2)}) %collective-permute-start.40) | collective-permute-done | bytes 589856 | tf_op jit(solution)/shard_map/ppermute | solution.py:315
  531.2 23.5 %collective-permute-done.36.got_ref = bf16[2,192,768]{2,1,0:T(8,128)(2,1)} collective-permute-done((bf16[2,192,768]{2,1,0:T(8,128)(2,1)}, bf16[2,192,768]{2,1,0:T(8,128)(2,1)}, u32[]{:S(2)}, u32[]{:S(2)}) %collective-permute-start.36) | collective-permute-done | bytes 589856 | tf_op jit(solution)/shard_map/ppermute | solution.py:315
  573.3 26.6 %collective-permute-done.48.far_ref = bf16[1,768,768]{2,1,0:T(8,128)(2,1)} collective-permute-done((bf16[1,768,768]{2,1,0:T(8,128)(2,1)}, bf16[1,768,768]{2,1,0:T(8,128)(2,1)}, u32[]{:S(2)}, u32[]{:S(2)}) %collective-permute-start.48) | collective-permute-done | bytes 1179680 | tf_op jit(solution)/shard_map/ppermute | solution.py:315
  599.9 12.5 %collective-permute-done.43.far_ref = bf16[2,192,768]{2,1,0:T(8,128)(2,1)S(1)} collective-permute-done((bf16[2,192,768]{2,1,0:T(8,128)(2,1)}, bf16[2,192,768]{2,1,0:T(8,128)(2,1)S(1)}, u32[]{:S(2)}, u32[]{:S(2)}) %collective-permute-start.43) | collective-permute-done | bytes 589856 | tf_op jit(solution)/shard_map/ppermute | solution.py:315
  612.9 9.9 %collective-permute-done.45.far_ref = bf16[2,192,768]{2,1,0:T(8,128)(2,1)S(1)} collective-permute-done((bf16[2,192,768]{2,1,0:T(8,128)(2,1)}, bf16[2,192,768]{2,1,0:T(8,128)(2,1)S(1)}, u32[]{:S(2)}, u32[]{:S(2)}) %collective-permute-start.45) | collective-permute-done | bytes 589856 | tf_op jit(solution)/shard_map/ppermute | solution.py:315
  (140 shorter events, 167.8 us)
Async XLA Ops:
  183.6 58.7 %collective-permute-start.3 = (bf16[2,192,768]{2,1,0:T(8,128)(2,1)}, bf16[2,192,768]{2,1,0:T(8,128)(2,1)}, u32[]{:S(2)}, u32[]{:S(2)}) collective-permute-start(bf16[2,192,768]{2,1,0:T(8,128)(2,1)} %get-tuple-element.182), channel_id=1, source_target_pairs={{0,1},{1,0},{2,3},{3,2},{4,5},{5,4},{6,7},{7,6}} | collective-permute-start | bytes 1769480 | tf_op jit(solution)/shard_map/ppermute | solution.py:315
  198.1 45.9 %collective-permute-start.9 = (bf16[2,192,768]{2,1,0:T(8,128)(2,1)}, bf16[2,192,768]{2,1,0:T(8,128)(2,1)}, u32[]{:S(2)}, u32[]{:S(2)}) collective-permute-start(bf16[2,192,768]{2,1,0:T(8,128)(2,1)} %collective-permute-done.8.far_ref), channel_id=1, source_target_pairs={{0,1},{1,0},{2,3},{3,2},{4,5},{5,4},{6,7},{7,6}} | collective-permute-start | bytes 1769480 | tf_op jit(solution)/shard_map/ppermute | solution.py:315
  198.1 44.2 %collective-permute-start.15 = (bf16[2,192,768]{2,1,0:T(8,128)(2,1)}, bf16[2,192,768]{2,1,0:T(8,128)(2,1)}, u32[]{:S(2)}, u32[]{:S(2)}) collective-permute-start(bf16[2,192,768]{2,1,0:T(8,128)(2,1)} %get-tuple-element.197), channel_id=1, source_target_pairs={{0,2},{1,3},{2,0},{3,1},{4,6},{5,7},{6,4},{7,5}} | collective-permute-start | bytes 1769480 | tf_op jit(solution)/shard_map/ppermute | solution.py:315
  241.8 45.7 %collective-permute-start.14 = (bf16[2,192,768]{2,1,0:T(8,128)(2,1)}, bf16[2,192,768]{2,1,0:T(8,128)(2,1)}, u32[]{:S(2)}, u32[]{:S(2)}) collective-permute-start(bf16[2,192,768]{2,1,0:T(8,128)(2,1)} %get-tuple-element.197), channel_id=1, source_target_pairs={{0,1},{1,0},{2,3},{3,2},{4,5},{5,4},{6,7},{7,6}} | collective-permute-start | bytes 1769480 | tf_op jit(solution)/shard_map/ppermute | solution.py:315
  242.3 45.2 %collective-permute-start.16 = (bf16[2,192,768]{2,1,0:T(8,128)(2,1)}, bf16[2,192,768]{2,1,0:T(8,128)(2,1)}, u32[]{:S(2)}, u32[]{:S(2)}) collective-permute-start(bf16[2,192,768]{2,1,0:T(8,128)(2,1)} %collective-permute-done.15.far_ref), channel_id=1, source_target_pairs={{0,1},{1,0},{2,3},{3,2},{4,5},{5,4},{6,7},{7,6}} | collective-permute-start | bytes 1769480 | tf_op jit(solution)/shard_map/ppermute | solution.py:315
  242.3 39.1 %collective-permute-start.11 = (bf16[2,192,768]{2,1,0:T(8,128)(2,1)}, bf16[2,192,768]{2,1,0:T(8,128)(2,1)S(1)}, u32[]{:S(2)}, u32[]{:S(2)}) collective-permute-start(bf16[2,192,768]{2,1,0:T(8,128)(2,1)} %sum_far.13), channel_id=1, source_target_pairs={{0,2},{1,3},{2,0},{3,1},{4,6},{5,7},{6,4},{7,5}} | collective-permute-start | bytes 1769480 | tf_op jit(solution)/shard_map/ppermute | solution.py:315
  307.2 41.3 %collective-permute-start.19 = (bf16[2,2,192,768]{3,2,1,0:T(8,128)(2,1)}, bf16[2,2,192,768]{3,2,1,0:T(8,128)(2,1)}, u32[]{:S(2)}, u32[]{:S(2)}) collective-permute-start(bf16[2,2,192,768]{3,2,1,0:T(8,128)(2,1)} %get-tuple-element.243), channel_id=1, source_target_pairs={{0,1},{1,0},{2,3},{3,2},{4,5},{5,4},{6,7},{7,6}} | collective-permute-start | bytes 3538952 | tf_op jit(solution)/shard_map/ppermute | solution.py:315
  307.3 44.4 %collective-permute-start.20 = (bf16[1,768,768]{2,1,0:T(8,128)(2,1)}, bf16[1,768,768]{2,1,0:T(8,128)(2,1)}, u32[]{:S(2)}, u32[]{:S(2)}) collective-permute-start(bf16[1,768,768]{2,1,0:T(8,128)(2,1)} %sum_far.14), channel_id=1, source_target_pairs={{0,2},{1,3},{2,0},{3,1},{4,6},{5,7},{6,4},{7,5}} | collective-permute-start | bytes 3538952 | tf_op jit(solution)/shard_map/ppermute | solution.py:315
  309.0 72.0 %collective-permute-start.12 = (bf16[2,192,768]{2,1,0:T(8,128)(2,1)}, bf16[2,192,768]{2,1,0:T(8,128)(2,1)}, u32[]{:S(2)}, u32[]{:S(2)}) collective-permute-start(bf16[2,192,768]{2,1,0:T(8,128)(2,1)} %get-tuple-element.234), channel_id=1, source_target_pairs={{0,1},{1,0},{2,3},{3,2},{4,5},{5,4},{6,7},{7,6}} | collective-permute-start | bytes 1769480 | tf_op jit(solution)/shard_map/ppermute | solution.py:315
  309.2 39.4 %collective-permute-start.22 = (bf16[2,192,768]{2,1,0:T(8,128)(2,1)}, bf16[2,192,768]{2,1,0:T(8,128)(2,1)}, u32[]{:S(2)}, u32[]{:S(2)}) collective-permute-start(bf16[2,192,768]{2,1,0:T(8,128)(2,1)} %get-tuple-element.234), channel_id=1, source_target_pairs={{0,2},{1,3},{2,0},{3,1},{4,6},{5,7},{6,4},{7,5}} | collective-permute-start | bytes 1769480 | tf_op jit(solution)/shard_map/ppermute | solution.py:315
  328.9 49.1 %collective-permute-start.21 = (bf16[2,2,192,768]{3,2,1,0:T(8,128)(2,1)}, bf16[2,2,192,768]{3,2,1,0:T(8,128)(2,1)}, u32[]{:S(2)}, u32[]{:S(2)}) collective-permute-start(bf16[2,2,192,768]{3,2,1,0:T(8,128)(2,1)} %get-tuple-element.250), channel_id=1, source_target_pairs={{0,1},{1,0},{2,3},{3,2},{4,5},{5,4},{6,7},{7,6}} | collective-permute-start | bytes 3538952 | tf_op jit(solution)/shard_map/ppermute | solution.py:315
  434.9 51.8 %collective-permute-start.30 = (bf16[2,1,768,768]{3,2,1,0:T(8,128)(2,1)}, bf16[2,1,768,768]{3,2,1,0:T(8,128)(2,1)}, u32[]{:S(2)}, u32[]{:S(2)}) collective-permute-start(bf16[2,1,768,768]{3,2,1,0:T(8,128)(2,1)} %bitcast.18), channel_id=1, source_target_pairs={{0,1},{1,0},{2,3},{3,2},{4,5},{5,4},{6,7},{7,6}} | collective-permute-start | bytes 7077896 | tf_op jit(solution)/shard_map/ppermute | solution.py:315
  435.2 41.3 %collective-permute-start.28 = (bf16[2,2,192,768]{3,2,1,0:T(8,128)(2,1)}, bf16[2,2,192,768]{3,2,1,0:T(8,128)(2,1)}, u32[]{:S(2)}, u32[]{:S(2)}) collective-permute-start(bf16[2,2,192,768]{3,2,1,0:T(8,128)(2,1)} %get-tuple-element.263), channel_id=1, source_target_pairs={{0,1},{1,0},{2,3},{3,2},{4,5},{5,4},{6,7},{7,6}} | collective-permute-start | bytes 3538952 | tf_op jit(solution)/shard_map/ppermute | solution.py:315
  435.5 45.9 %collective-permute-start.27 = (bf16[1,768,768]{2,1,0:T(8,128)(2,1)}, bf16[1,768,768]{2,1,0:T(8,128)(2,1)}, u32[]{:S(2)}, u32[]{:S(2)}) collective-permute-start(bf16[1,768,768]{2,1,0:T(8,128)(2,1)} %get-tuple-element.253), channel_id=1, source_target_pairs={{0,1},{1,0},{2,3},{3,2},{4,5},{5,4},{6,7},{7,6}} | collective-permute-start | bytes 3538952 | tf_op jit(solution)/shard_map/ppermute | solution.py:315
  435.7 40.5 %collective-permute-start.29 = (bf16[2,192,768]{2,1,0:T(8,128)(2,1)S(1)}, bf16[2,192,768]{2,1,0:T(8,128)(2,1)}, u32[]{:S(2)}, u32[]{:S(2)}) collective-permute-start(bf16[2,192,768]{2,1,0:T(8,128)(2,1)S(1)} %copy-done.5), channel_id=1, source_target_pairs={{0,2},{1,3},{2,0},{3,1},{4,6},{5,7},{6,4},{7,5}} | collective-permute-start | bytes 1769480 | tf_op jit(solution)/shard_map/ppermute | solution.py:315
  464.1 54.0 %collective-permute-start.32 = (bf16[1,768,768]{2,1,0:T(8,128)(2,1)}, bf16[1,768,768]{2,1,0:T(8,128)(2,1)}, u32[]{:S(2)}, u32[]{:S(2)}) collective-permute-start(bf16[1,768,768]{2,1,0:T(8,128)(2,1)} %collective-permute-done.31.far_ref), channel_id=1, source_target_pairs={{0,1},{1,0},{2,3},{3,2},{4,5},{5,4},{6,7},{7,6}} | collective-permute-start | bytes 3538952 | tf_op jit(solution)/shard_map/ppermute | solution.py:315
  492.7 70.5 %collective-permute-start.42 = (bf16[1,768,768]{2,1,0:T(8,128)(2,1)}, bf16[1,768,768]{2,1,0:T(8,128)(2,1)}, u32[]{:S(2)}, u32[]{:S(2)}) collective-permute-start(bf16[1,768,768]{2,1,0:T(8,128)(2,1)} %sum_far.19), channel_id=1, source_target_pairs={{0,2},{1,3},{2,0},{3,1},{4,6},{5,7},{6,4},{7,5}} | collective-permute-start | bytes 3538952 | tf_op jit(solution)/shard_map/ppermute | solution.py:315
  505.4 49.2 %collective-permute-start.36 = (bf16[2,192,768]{2,1,0:T(8,128)(2,1)}, bf16[2,192,768]{2,1,0:T(8,128)(2,1)}, u32[]{:S(2)}, u32[]{:S(2)}) collective-permute-start(bf16[2,192,768]{2,1,0:T(8,128)(2,1)} %sum_far.18), channel_id=1, source_target_pairs={{0,2},{1,3},{2,0},{3,1},{4,6},{5,7},{6,4},{7,5}} | collective-permute-start | bytes 1769480 | tf_op jit(solution)/shard_map/ppermute | solution.py:315
  518.1 41.9 %collective-permute-start.39 = (bf16[2,192,768]{2,1,0:T(8,128)(2,1)}, bf16[2,192,768]{2,1,0:T(8,128)(2,1)}, u32[]{:S(2)}, u32[]{:S(2)}) collective-permute-start(bf16[2,192,768]{2,1,0:T(8,128)(2,1)} %get-tuple-element.287), channel_id=1, source_target_pairs={{0,1},{1,0},{2,3},{3,2},{4,5},{5,4},{6,7},{7,6}} | collective-permute-start | bytes 1769480 | tf_op jit(solution)/shard_map/ppermute | solution.py:315
  518.1 41.9 %collective-permute-start.41 = (bf16[2,192,768]{2,1,0:T(8,128)(2,1)}, bf16[2,192,768]{2,1,0:T(8,128)(2,1)}, u32[]{:S(2)}, u32[]{:S(2)}) collective-permute-start(bf16[2,192,768]{2,1,0:T(8,128)(2,1)} %collective-permute-done.40.far_ref), channel_id=1, source_target_pairs={{0,1},{1,0},{2,3},{3,2},{4,5},{5,4},{6,7},{7,6}} | collective-permute-start | bytes 1769480 | tf_op jit(solution)/shard_map/ppermute | solution.py:315
  571.0 41.4 %collective-permute-start.43 = (bf16[2,192,768]{2,1,0:T(8,128)(2,1)}, bf16[2,192,768]{2,1,0:T(8,128)(2,1)S(1)}, u32[]{:S(2)}, u32[]{:S(2)}) collective-permute-start(bf16[2,192,768]{2,1,0:T(8,128)(2,1)} %get-tuple-element.298), channel_id=1, source_target_pairs={{0,2},{1,3},{2,0},{3,1},{4,6},{5,7},{6,4},{7,5}} | collective-permute-start | bytes 1769480 | tf_op jit(solution)/shard_map/ppermute | solution.py:315
  572.7 39.7 %collective-permute-start.38 = (bf16[2,192,768]{2,1,0:T(8,128)(2,1)}, bf16[2,192,768]{2,1,0:T(8,128)(2,1)S(1)}, u32[]{:S(2)}, u32[]{:S(2)}) collective-permute-start(bf16[2,192,768]{2,1,0:T(8,128)(2,1)} %get-tuple-element.298), channel_id=1, source_target_pairs={{0,1},{1,0},{2,3},{3,2},{4,5},{5,4},{6,7},{7,6}} | collective-permute-start | bytes 1769480 | tf_op jit(solution)/shard_map/ppermute | solution.py:315
  572.7 50.1 %collective-permute-start.45 = (bf16[2,192,768]{2,1,0:T(8,128)(2,1)}, bf16[2,192,768]{2,1,0:T(8,128)(2,1)S(1)}, u32[]{:S(2)}, u32[]{:S(2)}) collective-permute-start(bf16[2,192,768]{2,1,0:T(8,128)(2,1)} %get-tuple-element.309), channel_id=1, source_target_pairs={{0,2},{1,3},{2,0},{3,1},{4,6},{5,7},{6,4},{7,5}} | collective-permute-start | bytes 1769480 | tf_op jit(solution)/shard_map/ppermute | solution.py:315
  573.1 57.1 %collective-permute-start.47 = (bf16[1,768,768]{2,1,0:T(8,128)(2,1)}, bf16[1,768,768]{2,1,0:T(8,128)(2,1)}, u32[]{:S(2)}, u32[]{:S(2)}) collective-permute-start(bf16[1,768,768]{2,1,0:T(8,128)(2,1)} %get-tuple-element.317), channel_id=1, source_target_pairs={{0,1},{1,0},{2,3},{3,2},{4,5},{5,4},{6,7},{7,6}} | collective-permute-start | bytes 3538952 | tf_op jit(solution)/shard_map/ppermute | solution.py:315
  (37 other events, 670.8 us)
